TPU v7x, 32 devices: a whole 2x2x4 slice. The times are simulated.
32 devices in a mesh: gx: 8 (over z, y), gy: 4 (over x, core).
Axes of the slice: x: 2, y: 2, z: 4, core: 2. Of those that a mesh axis runs over, the one named last changes fastest.
Arguments:
- right_side: float32 [64, 128, 128], P('gy', 'gx'), may hold values from -6 to 9
- diagonal: float32 [64, 128, 128], P('gy', 'gx'), may hold values from 0.02 to 0.5
- horizontal: float32 [64, 128, 128], P('gy', 'gx'), may hold values from 0.1 to 1
- vertical: float32 [128], replicated, may hold values from 0.2 to 2
- precond: float32 [2, 128, 128], replicated, may hold values from -4 to 4
- edge_rows: int32 [2, 64], replicated, may hold values from 0 to 63, as said below
Outputs:
- solution_field: float32 [64, 128, 128], P('gy', 'gx')
- residual: float32 [64, 128, 128], P('gy', 'gx')
- residual_sq: float32 [3], replicated
Inputs may be any that keep to these rules, and one draw needn't show every extreme that they name: Each row of edge_rows lists every number 0 to 63 exactly once.
All inputs are finite; a program needn't handle non-finite values.
Results may differ from a plain program's by a relative error of at most 0.00014.
Values sent between devices are 32-bit elements; how exact they have to be, the bound alone decides.
A program may use at most 64 MiB of HBM per device.

v0:
```python
import functools

import jax
import jax.numpy as jnp
from jax import lax
from jax.experimental import pallas as pl
from jax.experimental.pallas import tpu as pltpu
from jax.sharding import PartitionSpec as P

ITERS = 3
KEYS = [(i, j) for j in range(ITERS + 1) for i in range(j + 1)]
MESH = pl.DeviceIdType.MESH
ANY = pl.BlockSpec(memory_space=pl.ANY)
VMEM = pl.BlockSpec(memory_space=pltpu.VMEM)


def kernel(
    n_gx,
    n_gy,
    out_rows,
    edge_table,
    right_side,
    diagonal,
    horizontal,
    vertical,
    precond,
    fields,
    images,
    out_totals,
    r0,
    diag,
    horiz,
    vert,
    matrix,
    send_cols,
    pack,
    from_east,
    from_west,
    from_north,
    from_south,
    far_pack,
    near_pack,
    far_z,
    near_z,
    gathered,
    strip,
    outside,
    partial,
    sums,
    edge_rows,
    load_sem,
    col_send,
    east_recv,
    west_recv,
    far_send,
    far_recv,
    near_send,
    near_recv,
    row_send,
    north_recv,
    south_recv,
    sum_send,
    sum_recv,
):
    rows, levels = out_rows, r0.shape[-1]
    cells = r0.shape[0]
    cols = cells // rows
    tall = n_gy * rows
    gx, gy = lax.axis_index("gx"), lax.axis_index("gy")
    n_all = n_gx * n_gy
    half = n_gx // 2
    me = gx * n_gy + gy

    def for_others(visit):
        def step(i, carry):
            for j in range(n_gy):
                visit(lax.rem(gx + i, n_gx), lax.rem(gy + j, n_gy))
            return carry

        if n_all <= 64:
            for i in sorted(range(1, n_gx), key=lambda i: min(i, n_gx - i)):
                step(i, 0)
        else:
            lax.fori_loop(1, n_gx, step, 0)
        for j in range(1, n_gy):
            visit(gx, lax.rem(gy + j, n_gy))

    barrier = pltpu.get_barrier_semaphore()

    def greet(x, y):
        pl.semaphore_signal(barrier, inc=1, device_id=(x, y), device_id_type=MESH)

    for_others(greet)

    panel = lax.convert_element_type(gx >= half, jnp.int32)
    loads = [
        pltpu.make_async_copy(right_side, r0, load_sem.at[0]),
        pltpu.make_async_copy(precond.at[panel], matrix.at[pl.ds(0, levels)], load_sem.at[1]),
        pltpu.make_async_copy(horizontal, horiz, load_sem.at[2]),
        pltpu.make_async_copy(diagonal, diag, load_sem.at[3]),
        pltpu.make_async_copy(vertical, vert, load_sem.at[4]),
        pltpu.make_async_copy(edge_table, edge_rows, load_sem.at[5]),
        pltpu.make_async_copy(precond.at[1 - panel], matrix.at[pl.ds(levels, levels)], load_sem.at[6]),
    ]
    for load in loads:
        load.start()

    east_x, west_x = lax.rem(gx + 1, n_gx), lax.rem(gx + n_gx - 1, n_gx)
    east_border = (gx == half - 1) | (gx == n_gx - 1)
    west_border = (gx == half) | (gx == 0)
    border = east_border | west_border
    far_x = jnp.where(east_border, east_x, west_x)
    side = jnp.where(east_border, 0, 1)
    table = jnp.where((gx == half - 1) | (gx == half), 0, 1)
    edge_cols = [
        pl.ds(jnp.where(east_border, cols - 1 - i, i), rows, stride=cols) for i in range(3)
    ]
    first_row = pl.multiple_of(gy * rows, rows)
    own = pl.ds(first_row, rows)
    has_north, has_south = gy < n_gy - 1, gy > 0

    @pl.when(jnp.logical_not(has_north))
    def _():
        from_north[...] = jnp.zeros_like(from_north)

    @pl.when(jnp.logical_not(has_south))
    def _():
        from_south[...] = jnp.zeros_like(from_south)

    outside[...] = jnp.zeros_like(outside)

    def precondition(v, panels=1):
        return lax.dot_general(
            v,
            matrix[pl.ds(0, panels * levels), :],
            (((1,), (1,)), ((), ())),
            precision=lax.Precision.HIGHEST,
            preferred_element_type=jnp.float32,
        )

    def col_copy(t, side):
        buffer, recv, x = (
            (from_west, west_recv, east_x) if side == 0 else (from_east, east_recv, west_x)
        )
        return pltpu.make_async_remote_copy(
            src_ref=send_cols.at[t, pl.ds(side * rows, rows)],
            dst_ref=buffer.at[t],
            send_sem=col_send.at[t, side],
            recv_sem=recv.at[t],
            device_id=(x, gy),
            device_id_type=MESH,
        )

    def far_copy(t, g):
        return pltpu.make_async_remote_copy(
            src_ref=pack.at[pl.ds(0, 3)] if t == 0 else pack.at[3 + t],
            dst_ref=far_pack.at[:, own] if t == 0 else far_z.at[t - 1, own],
            send_sem=far_send.at[t],
            recv_sem=far_recv.at[t],
            device_id=(far_x, g),
            device_id_type=MESH,
        )

    def near_copy(t, g):
        return pltpu.make_async_remote_copy(
            src_ref=pack.at[pl.ds(0, 4)] if t == 0 else pack.at[3 + t],
            dst_ref=near_pack.at[:, own] if t == 0 else near_z.at[own],
            send_sem=near_send.at[t],
            recv_sem=near_recv.at[t],
            device_id=(gx, g),
            device_id_type=MESH,
        )

    def row_copy(t, side):
        buffer, recv, y, row = (
            (from_south, south_recv, gy + 1, cells - cols)
            if side == 0
            else (from_north, north_recv, gy - 1, 0)
        )
        return pltpu.make_async_remote_copy(
            src_ref=fields.at[t, pl.ds(row, cols)],
            dst_ref=buffer.at[t],
            send_sem=row_send.at[t, side],
            recv_sem=recv.at[t],
            device_id=(gx, y),
            device_id_type=MESH,
        )

    def send_cols_on(t, edges):
        send_cols[t] = precondition(edges)

        @pl.when(border)
        def _():
            edge = send_cols[t, pl.ds(side * rows, rows), :]
            if t == 0:
                items = [
                    edge,
                    horiz[edge_cols[0], :],
                    diag[edge_cols[0], :],
                    horiz[edge_cols[1], :],
                ]
                for k, item in enumerate(items):
                    pack[k] = item
                    near_pack[k, own, :] = item
            else:
                pack[3 + t] = edge
                if t == 1:
                    near_z[own, :] = edge

        if t == 0:
            pl.semaphore_wait(barrier, n_all - 1)

        @pl.when(border)
        def _():
            for j in sorted(range(n_gy), key=lambda j: abs(2 * j - n_gy)):
                far_copy(t, lax.rem(gy + j, n_gy)).start()
            if t < 2:
                for j in range(1, n_gy):
                    near_copy(t, lax.rem(gy + j, n_gy)).start()

        @pl.when(jnp.logical_not(east_border))
        def _():
            col_copy(t, 0).start()

        @pl.when(jnp.logical_not(west_border))
        def _():
            col_copy(t, 1).start()

    def send_rows(t):
        @pl.when(has_north)
        def _():
            row_copy(t, 0).start()

        @pl.when(has_south)
        def _():
            row_copy(t, 1).start()

    def receive_rows(t):
        @pl.when(has_north)
        def _():
            row_copy(t, 1).wait_recv()

        @pl.when(has_south)
        def _():
            row_copy(t, 0).wait_recv()

    def receive_cols(t):
        @pl.when(jnp.logical_not(east_border))
        def _():
            col_copy(t, 1).wait_recv()
            outside[pl.ds(0, rows), :] = from_east[t]

        @pl.when(jnp.logical_not(west_border))
        def _():
            col_copy(t, 0).wait_recv()
            outside[pl.ds(rows, rows), :] = from_west[t]

    col_id = lax.rem(lax.broadcasted_iota(jnp.int32, (cells, levels), 0), cols)
    east_edge = pl.ds(cols - 1, rows, stride=cols)
    west_edge = pl.ds(0, rows, stride=cols)
    south_edge = pl.ds(0, cols)
    north_edge = pl.ds(cells - cols, cols)

    def edge_columns(ref):
        return jnp.concatenate([ref[east_edge, :], ref[west_edge, :]], 0)

    def column_part(z):
        lane = lax.broadcasted_iota(jnp.int32, z.shape, 1)
        up = jnp.where(lane < levels - 1, pltpu.roll(z, levels - 1, 1), 0.0)
        down = jnp.where(lane > 0, pltpu.roll(z, 1, 1), 0.0)
        return vert[...] * (2.0 * z - (up + down))

    def inner_image(z):
        east = jnp.where(col_id < cols - 1, pltpu.roll(z, cells - 1, 0), 0.0)
        west = jnp.where(col_id > 0, pltpu.roll(z, 1, 0), 0.0)
        none = jnp.zeros((cols, levels), jnp.float32)
        north = jnp.concatenate([z[cols:], none], 0)
        south = jnp.concatenate([none, z[:-cols]], 0)
        beside = east + west + north + south
        return diag[...] * z + horiz[...] * (4.0 * z - beside) + column_part(z)

    def product(a, b):
        both = (a * b).reshape(-1, 8, levels)
        return jnp.sum(jnp.sum(both, axis=0), axis=0, keepdims=True)

    tall_id = lax.broadcasted_iota(jnp.int32, (tall, levels), 0)

    def along(w):
        north = jnp.where(tall_id < tall - 1, pltpu.roll(w, tall - 1, 0), 0.0)
        south = jnp.where(tall_id > 0, pltpu.roll(w, 1, 0), 0.0)
        return north + south

    def stencil(w, d, h):
        return d * w + h * (4.0 * w - along(w)) + column_part(w)

    def gather_rows(start, count, pairs):
        def one(y):
            row = edge_rows[table, start + y]
            for dst, src in pairs:
                gathered[dst, pl.ds(y, 1), :] = src[pl.ds(row, 1), :]

        if count <= 64:
            for y in range(count):
                one(y)
        else:

            def body(y, carry):
                one(y)
                return carry

            lax.fori_loop(0, count, body, 0)

    def wait_bytes(ref, sem):
        pltpu.make_async_copy(ref, ref, sem).wait()

    near_rest = pl.ds(0, (n_gy - 1) * rows)

    def correct_first():
        wait_bytes(far_pack, far_recv.at[0])
        wait_bytes(near_pack.at[:, near_rest], near_recv.at[0])
        gather_rows(0, tall, [(0, far_pack.at[0]), (1, near_pack.at[0])])
        b_near = -(near_pack[1] * gathered[0])
        b_far = -(far_pack[1] * gathered[1])
        strip[0] = b_near
        both = precondition(jnp.concatenate([b_near, b_far], 0), 2)
        strip[1] = both[:tall, :levels]
        strip[2] = both[tall:, levels:]

    def correct_second():
        wait_bytes(far_z.at[0], far_recv.at[1])
        wait_bytes(near_z.at[near_rest], near_recv.at[1])
        w_near, w_far = strip[1], strip[2]
        strip[3] = far_z[0] + w_far
        strip[4] = near_z[...] + w_near
        gather_rows(0, tall, [(0, strip.at[3]), (1, strip.at[4])])
        h_near, h_far = near_pack[1], far_pack[1]
        b_near = stencil(w_near, near_pack[2], h_near) - h_near * gathered[0]
        b_far = stencil(w_far, far_pack[2], h_far) - h_far * gathered[1]
        b_next = -(near_pack[3] * w_near)
        all_three = precondition(jnp.concatenate([b_near, b_next, b_far], 0), 2)
        w_edge, w_next = all_three[:tall, :levels], all_three[tall : 2 * tall, :levels]
        strip[3] = b_near
        strip[4] = b_next
        strip[5] = all_three[2 * tall :, levels:]
        strip[6] = w_edge
        strip[7] = w_next
        strip[8] = along(w_next)
        strip[9] = stencil(w_edge, near_pack[2], h_near) - h_near * w_next

    def correct_third():
        c0, c1, c2 = edge_cols
        w_edge, w_next, beside = strip[6, own, :], strip[7, own, :], strip[8, own, :]
        h1 = horiz[c1, :]
        later = diag[c1, :] * w_next + h1 * (4.0 * w_next - beside - w_edge) + column_part(w_next)
        b_third = -(horiz[c2, :] * w_next)
        gather_rows(first_row, rows, [(2, strip.at[5])])
        wait_bytes(far_z.at[1], far_recv.at[2])
        gather_rows(first_row, rows, [(3, far_z.at[1])])
        across = gathered[2, pl.ds(0, rows), :] + gathered[3, pl.ds(0, rows), :]
        b_edge = strip[9, own, :] - horiz[c0, :] * across
        none = jnp.zeros((rows, levels), jnp.float32)
        changes = [
            [strip[0, own, :], none, none],
            [strip[3, own, :], strip[4, own, :], none],
            [b_edge, later, b_third],
        ]
        before = [jnp.concatenate([r0[c, :] for c in edge_cols], 0)]
        after = [before[0]]
        for t in range(ITERS):
            old = jnp.concatenate([images[t, c, :] for c in edge_cols], 0)
            new = old + jnp.concatenate(changes[t], 0)
            before.append(old)
            after.append(new)
            for k in range(t + 1):
                images[t, edge_cols[k], :] = new[k * rows : (k + 1) * rows]
        for k, (i, j) in enumerate(KEYS):
            if j > 0:
                partial[pl.ds(k, 1), :] += product(after[i], after[j]) - product(before[i], before[j])

    for load in loads:
        load.wait()
    terms = {}
    spaces = [r0]
    send_cols_on(0, edge_columns(r0))
    edge_horiz = edge_columns(horiz)
    for t in range(ITERS):
        image = images.at[t]
        z = precondition(spaces[-1][...])
        fields[t] = z
        send_rows(t)
        newest = len(spaces) - 1
        for i in range(len(spaces)):
            terms[(i, newest)] = product(spaces[i][...], spaces[newest][...])
        image[...] = inner_image(z)
        receive_rows(t)
        image[south_edge, :] = image[south_edge, :] - horiz[south_edge, :] * from_south[t]
        image[north_edge, :] = image[north_edge, :] - horiz[north_edge, :] * from_north[t]
        inside = edge_columns(image)
        receive_cols(t)
        edges = inside - edge_horiz * outside[...]
        if t < ITERS - 1:
            send_cols_on(t + 1, edges)
        image[east_edge, :] = edges[:rows]
        image[west_edge, :] = edges[rows:]
        spaces.append(image)
    newest = len(spaces) - 1
    for i in range(len(spaces)):
        terms[(i, newest)] = product(spaces[i][...], spaces[newest][...])
    for k, key in enumerate(KEYS):
        partial[pl.ds(k, 1), :] = terms[key]

    @pl.when(border)
    def _():
        correct_first()
        correct_second()
        correct_third()

    height = -(-len(KEYS) // 8) * 8
    row_id = lax.broadcasted_iota(jnp.int32, (height, levels), 0)
    lane = lax.broadcasted_iota(jnp.int32, (height, levels), 1)
    stacked = jnp.where(row_id < len(KEYS), partial[...], 0.0)
    summed = jnp.sum(stacked, axis=1, keepdims=True)
    sums[me] = jnp.sum(jnp.where(lane == row_id, summed, 0.0), axis=0, keepdims=True)

    def tell(x, y):
        pltpu.make_async_remote_copy(
            src_ref=sums.at[me],
            dst_ref=sums.at[me],
            send_sem=sum_send,
            recv_sem=sum_recv,
            device_id=(x, y),
            device_id_type=MESH,
        ).start()

    for_others(tell)
    for t in range(ITERS):

        @pl.when(jnp.logical_not(east_border))
        def _(t=t):
            col_copy(t, 0).wait_send()

        @pl.when(jnp.logical_not(west_border))
        def _(t=t):
            col_copy(t, 1).wait_send()

        @pl.when(has_north)
        def _(t=t):
            row_copy(t, 0).wait_send()

        @pl.when(has_south)
        def _(t=t):
            row_copy(t, 1).wait_send()

    @pl.when(border)
    def _():
        wait_bytes(far_pack, far_send.at[0])
        wait_bytes(far_z.at[0], far_send.at[1])
        wait_bytes(far_z.at[1], far_send.at[2])
        wait_bytes(near_pack.at[:, near_rest], near_send.at[0])
        wait_bytes(near_z.at[near_rest], near_send.at[1])
        c0, c1, c2 = edge_cols
        fields[1, c0, :] += strip[1, own, :]
        fields[2, c0, :] += strip[6, own, :]
        fields[2, c1, :] += strip[7, own, :]

    others = sums.at[pl.ds(0, n_all - 1)]
    wait_bytes(others, sum_recv)
    out_totals[...] = jnp.sum(sums[...], axis=0)
    wait_bytes(others, sum_send)


def finish(total_cells, all_totals, r0, fields, images, out_x, out_r, out_norms, x, r, sem):
    levels = r0.shape[-1]
    totals = all_totals[...]
    value = {key: totals[:, k : k + 1] for k, key in enumerate(KEYS)}

    rho, g0, g1, g2 = value[(0, 0)], value[(0, 1)], value[(0, 2)], value[(0, 3)]
    a00, a01, a02 = value[(1, 1)], value[(1, 2)], value[(1, 3)]
    a11, a12, a22 = value[(2, 2)], value[(2, 3)], value[(3, 3)]
    l10, l20, y0 = a01 / a00, a02 / a00, g0 / a00
    d1, e12, f1 = a11 - l10 * a01, a12 - l10 * a02, g1 - l10 * g0
    l21, y1 = e12 / d1, f1 / d1
    d2, f2 = a22 - l20 * a02 - l21 * e12, g2 - l20 * g0 - l21 * f1
    y2 = f2 / d2
    norm0 = rho - y0 * g0
    norm1 = norm0 - y1 * f1
    norm2 = norm1 - y2 * f2
    y1 = y1 - l21 * y2
    y0 = y0 - l10 * y1 - l20 * y2
    norm_lane = lax.broadcasted_iota(jnp.int32, (1, levels), 1)
    norms = jnp.where(norm_lane == 0, norm0, jnp.where(norm_lane == 1, norm1, norm2))
    out_norms[...] = norms[:, :ITERS] / total_cells
    rows = r0.shape[0]
    pieces = 2 if rows % 16 == 0 else 1
    size = rows // pieces
    copies = []
    for p in range(pieces):
        span = pl.ds(p * size, size)
        x[span] = y0 * fields[0, span] + y1 * fields[1, span] + y2 * fields[2, span]
        r[span] = (
            r0[span] - y0 * images[0, span] - y1 * images[1, span] - y2 * images[2, span]
        )
        for k, (src, dst) in enumerate(((x, out_x), (r, out_r))):
            copy = pltpu.make_async_copy(src.at[span], dst.at[span], sem.at[p, k])
            copy.start()
            copies.append(copy)
    for copy in copies:
        copy.wait()


def on_device(n_gx, n_gy, right_side, diagonal, horizontal, vertical, precond, edge_rows):
    rows, cols, levels = right_side.shape
    f32 = jnp.float32
    block = (rows * cols, levels)
    column = (n_gy * rows, levels)
    sems = pltpu.SemaphoreType.DMA
    basis = pltpu.VMEM((ITERS,) + block, f32)
    fields, images, totals, start = pl.pallas_call(
        functools.partial(kernel, n_gx, n_gy, rows),
        out_shape=(basis, basis, pltpu.VMEM((1, levels), f32), pltpu.VMEM(block, f32)),
        in_specs=[ANY, ANY, ANY, ANY, ANY, ANY],
        out_specs=(VMEM, VMEM, VMEM, VMEM),
        scratch_shapes=[
            pltpu.VMEM(block, f32),
            pltpu.VMEM(block, f32),
            pltpu.VMEM((1, levels), f32),
            pltpu.VMEM((2 * levels, levels), f32),
            pltpu.VMEM((ITERS, 2 * rows, levels), f32),
            pltpu.VMEM((6, rows, levels), f32),
            pltpu.VMEM((ITERS, rows, levels), f32),
            pltpu.VMEM((ITERS, rows, levels), f32),
            pltpu.VMEM((ITERS, cols, levels), f32),
            pltpu.VMEM((ITERS, cols, levels), f32),
            pltpu.VMEM((3,) + column, f32),
            pltpu.VMEM((4,) + column, f32),
            pltpu.VMEM((2,) + column, f32),
            pltpu.VMEM(column, f32),
            pltpu.VMEM((4,) + column, f32),
            pltpu.VMEM((10,) + column, f32),
            pltpu.VMEM((2 * rows, levels), f32),
            pltpu.VMEM((16, levels), f32),
            pltpu.VMEM((n_gx * n_gy, 1, levels), f32),
            pltpu.SMEM(edge_rows.shape, jnp.int32),
            sems((7,)),
            sems((ITERS, 2)),
            sems((ITERS,)),
            sems((ITERS,)),
            sems((ITERS,)),
            sems((ITERS,)),
            sems((2,)),
            sems((2,)),
            sems((ITERS, 2)),
            sems((ITERS,)),
            sems((ITERS,)),
            sems(()),
            sems(()),
        ],
        compiler_params=pltpu.CompilerParams(collective_id=0, has_side_effects=True),
    )(
        edge_rows,
        right_side.reshape(block),
        diagonal.reshape(block),
        horizontal.reshape(block),
        vertical.reshape(1, levels),
        precond,
    )
    in_vmem = functools.partial(
        pltpu.with_memory_space_constraint, memory_space=pltpu.VMEM
    )
    total_cells = float(rows * cols * levels * n_gx * n_gy)
    x, r, norms = pl.pallas_call(
        functools.partial(finish, total_cells),
        out_shape=(
            jax.ShapeDtypeStruct(block, f32),
            jax.ShapeDtypeStruct(block, f32),
            jax.ShapeDtypeStruct((1, ITERS), f32),
        ),
        in_specs=[VMEM, VMEM, VMEM, VMEM],
        out_specs=(ANY, ANY, VMEM),
        scratch_shapes=[pltpu.VMEM(block, f32), pltpu.VMEM(block, f32), sems((2, 2))],
    )(in_vmem(totals), in_vmem(start), in_vmem(fields), in_vmem(images))
    shape = right_side.shape
    return x.reshape(shape), r.reshape(shape), norms.reshape(ITERS)


def solution(mesh):
    n_gx, n_gy = mesh.shape["gx"], mesh.shape["gy"]
    field = P("gy", "gx", None)
    return jax.shard_map(
        functools.partial(on_device, n_gx, n_gy),
        mesh=mesh,
        in_specs=(field, field, field, P(), P(), P()),
        out_specs=(field, field, P()),
        check_vma=False,
    )
```

profile of v0, /device:TPU:0, one launch (start us, length us, event | category | flops | bytes accessed | tf_op | source)
XLA Modules:
  0.0 25.4 jit_solution(11224633340567026765)
XLA Ops:
  0.6 22.8 %shard_map.85 = (f32[3,256,128]{2,1,0:T(8,128)S(1)}, f32[3,256,128]{2,1,0:T(8,128)S(1)}, f32[1,128]{1,0:T(1,128)S(1)}, f32[256,128]{1,0:T(8,128)S(1)}) custom-call(s32[2,64]{1,0:T(2,128)} %edge_table.1, f32[256,128]{1,0:T(8,128)} %bitcast.7, f32[256,128]{1,0:T(8,128)} %bitcast.8, f32[256,128]{1,0:T(8,128)} %bitcast.9, f32[1,128]{1,0:T(1,128)} %bitcast.10, ...), custom_call_target="tpu_custom_call" | custom-call | tf_op jit(solution)/shard_map/pallas_call | solution.py:518
  23.4 2.0 %shard_map.86 = (f32[256,128]{1,0:T(8,128)}, f32[256,128]{1,0:T(8,128)}, f32[1,3]{1,0:T(1,128)}) custom-call(f32[1,128]{1,0:T(1,128)S(1)} %get-tuple-element.10.all_totals, f32[256,128]{1,0:T(8,128)S(1)} %get-tuple-element.11.r0, f32[3,256,128]{2,1,0:T(8,128)S(1)} %get-tuple-element.12.fields, f32[3,256,128]{2,1,0:T(8,128)S(1)} %get-tuple-element.13.images), custom_call_target="tpu_custom_call" | custom-call | tf_op jit(solution)/shard_map/pallas_call | solution.py:571
where the time goes:
time: 25.5 us; the launch traced here: 25.4 us
  Pallas kernels  24.7 us (97%)
  between operations  0.64 us (3%)
    pallas_call x1, Pallas kernels, on_device(): pl.pallas_call(functools.partial(kernel, n_gx, n_gy, rows), out_shape=(ba...  22.8 us
    pallas_call x1, Pallas kernels, on_device(): pl.pallas_call(functools.partial(finish, total_cells), out_shape=(jax.Sha...  1.96 us

commit v1 on v0

--- a/solution.py
+++ b/solution.py
@@ -61,6 +61,8 @@
     south_recv,
     sum_send,
     sum_recv,
+    from_below,
+    from_above,
 ):
     rows, levels = out_rows, r0.shape[-1]
     cells = r0.shape[0]
@@ -71,6 +73,11 @@
     half = n_gx // 2
     me = gx * n_gy + gy
 
+    east_x, west_x = lax.rem(gx + 1, n_gx), lax.rem(gx + n_gx - 1, n_gx)
+    east_border = (gx == half - 1) | (gx == n_gx - 1)
+    west_border = (gx == half) | (gx == 0)
+    border = east_border | west_border
+
     def for_others(visit):
         def step(i, carry):
             for j in range(n_gy):
@@ -90,7 +97,39 @@
     def greet(x, y):
         pl.semaphore_signal(barrier, inc=1, device_id=(x, y), device_id_type=MESH)
 
-    for_others(greet)
+    span = max(n_gx // 4, 2)
+    n_spans = n_gx // span
+    place = gx // span
+    inside_span = lax.rem(gx, span)
+    lowest, highest = place == 0, place == n_spans - 1
+    greets_east = (inside_span == span - 1) & jnp.logical_not(east_border)
+    greets_west = (inside_span == 0) & jnp.logical_not(west_border)
+    for i in range(span):
+        for j in range(n_gy):
+            if i or j:
+                greet(place * span + lax.rem(inside_span + i, span), lax.rem(gy + j, n_gy))
+    for condition, x in (
+        (jnp.logical_not(lowest), gx - span),
+        (jnp.logical_not(highest), gx + span),
+        (greets_east, gx + 1),
+        (greets_west, gx - 1),
+    ):
+
+        @pl.when(condition)
+        def _(x=x):
+            greet(x, gy)
+
+    n_greets = span * n_gy - 1
+    for condition in (
+        jnp.logical_not(lowest),
+        jnp.logical_not(highest),
+        greets_east,
+        greets_west,
+    ):
+        n_greets = n_greets + lax.convert_element_type(condition, jnp.int32)
+
+    def hand_on(token, x):
+        pl.semaphore_signal(token, inc=1, device_id=(x, gy), device_id_type=MESH)
 
     panel = lax.convert_element_type(gx >= half, jnp.int32)
     loads = [
@@ -105,10 +144,36 @@
     for load in loads:
         load.start()
 
-    east_x, west_x = lax.rem(gx + 1, n_gx), lax.rem(gx + n_gx - 1, n_gx)
-    east_border = (gx == half - 1) | (gx == n_gx - 1)
-    west_border = (gx == half) | (gx == 0)
-    border = east_border | west_border
+    pl.semaphore_wait(barrier, n_greets)
+
+    @pl.when(jnp.logical_not(lowest))
+    def _():
+        pl.semaphore_wait(from_below, 1)
+
+    @pl.when(jnp.logical_not(highest))
+    def _():
+        hand_on(from_below, gx + span)
+
+    @pl.when(highest)
+    def _():
+        hand_on(from_above, gx - span)
+
+    far_stage = n_spans - 2 - place
+
+    def learn_above(t):
+        @pl.when(far_stage == t)
+        def _():
+            pl.semaphore_wait(from_above, 1)
+
+            @pl.when(jnp.logical_not(lowest))
+            def _():
+                hand_on(from_above, gx - span)
+
+            @pl.when(border)
+            def _():
+                for k in range(t + 1):
+                    send_far(k)
+
     far_x = jnp.where(east_border, east_x, west_x)
     side = jnp.where(east_border, 0, 1)
     table = jnp.where((gx == half - 1) | (gx == half), 0, 1)
@@ -207,24 +272,28 @@
                 if t == 1:
                     near_z[own, :] = edge
 
-        if t == 0:
-            pl.semaphore_wait(barrier, n_all - 1)
-
-        @pl.when(border)
-        def _():
-            for j in sorted(range(n_gy), key=lambda j: abs(2 * j - n_gy)):
-                far_copy(t, lax.rem(gy + j, n_gy)).start()
-            if t < 2:
+        @pl.when(border & (far_stage < t))
+        def _():
+            send_far(t)
+
+        @pl.when(jnp.logical_not(east_border))
+        def _():
+            col_copy(t, 0).start()
+
+        @pl.when(jnp.logical_not(west_border))
+        def _():
+            col_copy(t, 1).start()
+
+        if t < 2:
+
+            @pl.when(border)
+            def _():
                 for j in range(1, n_gy):
                     near_copy(t, lax.rem(gy + j, n_gy)).start()
 
-        @pl.when(jnp.logical_not(east_border))
-        def _():
-            col_copy(t, 0).start()
-
-        @pl.when(jnp.logical_not(west_border))
-        def _():
-            col_copy(t, 1).start()
+    def send_far(t):
+        for j in sorted(range(n_gy), key=lambda j: abs(2 * j - n_gy)):
+            far_copy(t, lax.rem(gy + j, n_gy)).start()
 
     def send_rows(t):
         @pl.when(has_north)
@@ -392,6 +461,7 @@
         for i in range(len(spaces)):
             terms[(i, newest)] = product(spaces[i][...], spaces[newest][...])
         image[...] = inner_image(z)
+        learn_above(t)
         receive_rows(t)
         image[south_edge, :] = image[south_edge, :] - horiz[south_edge, :] * from_south[t]
         image[north_edge, :] = image[north_edge, :] - horiz[north_edge, :] * from_north[t]
@@ -554,6 +624,8 @@
             sems((ITERS,)),
             sems(()),
             sems(()),
+            pltpu.SemaphoreType.REGULAR,
+            pltpu.SemaphoreType.REGULAR,
         ],
         compiler_params=pltpu.CompilerParams(collective_id=0, has_side_effects=True),
     )(

time: 25.5 us -> 26.8 us (1.051)
  Pallas kernels: 24.7 us -> 26 us
    pallas_call x1, Pallas kernels: 22.8 us -> 24.1 us  [on_device(): pl.pallas_call(functools.partial(kernel, n_gx, n_gy, rows), out_shape=(ba...]
where the time goes in v1:
time: 26.8 us; the launch traced here: 26.7 us
  Pallas kernels  26 us (97%)
  between operations  0.64 us (2%)
    pallas_call x1, Pallas kernels, on_device(): pl.pallas_call(functools.partial(kernel, n_gx, n_gy, rows), out_shape=(ba...  24.1 us
    pallas_call x1, Pallas kernels, on_device(): pl.pallas_call(functools.partial(finish, total_cells), out_shape=(jax.Sha...  1.96 us

profile of v1, /device:TPU:0, one launch (start us, length us, event | category | flops | bytes accessed | tf_op | source)
XLA Modules:
  0.0 26.7 jit_solution(14005710603747505912)
XLA Ops:
  0.6 24.1 %shard_map.85 = (f32[3,256,128]{2,1,0:T(8,128)S(1)}, f32[3,256,128]{2,1,0:T(8,128)S(1)}, f32[1,128]{1,0:T(1,128)S(1)}, f32[256,128]{1,0:T(8,128)S(1)}) custom-call(s32[2,64]{1,0:T(2,128)} %edge_table.1, f32[256,128]{1,0:T(8,128)} %bitcast.7, f32[256,128]{1,0:T(8,128)} %bitcast.8, f32[256,128]{1,0:T(8,128)} %bitcast.9, f32[1,128]{1,0:T(1,128)} %bitcast.10, ...), custom_call_target="tpu_custom_call" | custom-call | tf_op jit(solution)/shard_map/pallas_call | solution.py:588
  24.7 2.0 %shard_map.86 = (f32[256,128]{1,0:T(8,128)}, f32[256,128]{1,0:T(8,128)}, f32[1,3]{1,0:T(1,128)}) custom-call(f32[1,128]{1,0:T(1,128)S(1)} %get-tuple-element.10.all_totals, f32[256,128]{1,0:T(8,128)S(1)} %get-tuple-element.11.r0, f32[3,256,128]{2,1,0:T(8,128)S(1)} %get-tuple-element.12.fields, f32[3,256,128]{2,1,0:T(8,128)S(1)} %get-tuple-element.13.images), custom_call_target="tpu_custom_call" | custom-call | tf_op jit(solution)/shard_map/pallas_call | solution.py:643

commit v2 on v0

--- a/solution.py
+++ b/solution.py
@@ -32,16 +32,18 @@
     horiz,
     vert,
     matrix,
-    send_cols,
+    frame_z,
     pack,
+    mini_out,
+    mini_in,
+    wide,
     from_east,
     from_west,
     from_north,
     from_south,
     far_pack,
     near_pack,
-    far_z,
-    near_z,
+    far_last,
     gathered,
     strip,
     outside,
@@ -56,6 +58,8 @@
     far_recv,
     near_send,
     near_recv,
+    mini_send,
+    mini_recv,
     row_send,
     north_recv,
     south_recv,
@@ -143,7 +147,7 @@
             (from_west, west_recv, east_x) if side == 0 else (from_east, east_recv, west_x)
         )
         return pltpu.make_async_remote_copy(
-            src_ref=send_cols.at[t, pl.ds(side * rows, rows)],
+            src_ref=frame_z.at[t, pl.ds(side * rows, rows)],
             dst_ref=buffer.at[t],
             send_sem=col_send.at[t, side],
             recv_sem=recv.at[t],
@@ -153,32 +157,42 @@
 
     def far_copy(t, g):
         return pltpu.make_async_remote_copy(
-            src_ref=pack.at[pl.ds(0, 3)] if t == 0 else pack.at[3 + t],
-            dst_ref=far_pack.at[:, own] if t == 0 else far_z.at[t - 1, own],
+            src_ref=pack.at[pl.ds(0, 4)] if t == 0 else pack.at[5],
+            dst_ref=far_pack.at[:, own] if t == 0 else far_last.at[own],
             send_sem=far_send.at[t],
             recv_sem=far_recv.at[t],
             device_id=(far_x, g),
             device_id_type=MESH,
         )
 
-    def near_copy(t, g):
+    def near_copy(g):
         return pltpu.make_async_remote_copy(
-            src_ref=pack.at[pl.ds(0, 4)] if t == 0 else pack.at[3 + t],
-            dst_ref=near_pack.at[:, own] if t == 0 else near_z.at[own],
-            send_sem=near_send.at[t],
-            recv_sem=near_recv.at[t],
+            src_ref=pack.at[pl.ds(0, 5)],
+            dst_ref=near_pack.at[:, own],
+            send_sem=near_send,
+            recv_sem=near_recv,
             device_id=(gx, g),
             device_id_type=MESH,
         )
 
+    def mini_copy(side):
+        return pltpu.make_async_remote_copy(
+            src_ref=mini_out.at[side],
+            dst_ref=mini_in.at[side],
+            send_sem=mini_send.at[side],
+            recv_sem=mini_recv.at[side],
+            device_id=(gx, gy + 1 if side == 0 else gy - 1),
+            device_id_type=MESH,
+        )
+
     def row_copy(t, side):
         buffer, recv, y, row = (
-            (from_south, south_recv, gy + 1, cells - cols)
+            (from_south, south_recv, gy + 1, 2 * rows + cols)
             if side == 0
-            else (from_north, north_recv, gy - 1, 0)
+            else (from_north, north_recv, gy - 1, 2 * rows)
         )
         return pltpu.make_async_remote_copy(
-            src_ref=fields.at[t, pl.ds(row, cols)],
+            src_ref=frame_z.at[t, pl.ds(row, cols)],
             dst_ref=buffer.at[t],
             send_sem=row_send.at[t, side],
             recv_sem=recv.at[t],
@@ -186,54 +200,68 @@
             device_id_type=MESH,
         )
 
-    def send_cols_on(t, edges):
-        send_cols[t] = precondition(edges)
-
-        @pl.when(border)
-        def _():
-            edge = send_cols[t, pl.ds(side * rows, rows), :]
-            if t == 0:
-                items = [
-                    edge,
-                    horiz[edge_cols[0], :],
-                    diag[edge_cols[0], :],
-                    horiz[edge_cols[1], :],
-                ]
-                for k, item in enumerate(items):
-                    pack[k] = item
-                    near_pack[k, own, :] = item
-            else:
-                pack[3 + t] = edge
-                if t == 1:
-                    near_z[own, :] = edge
-
+    def for_rows(visit):
+        @pl.when(has_north)
+        def _():
+            visit(0)
+
+        @pl.when(has_south)
+        def _():
+            visit(1)
+
+    def fill_packs():
+        c0, c1, c2 = edge_cols
+        inward = 2 * (rows + cols)
+        items = [
+            frame_z[0, pl.ds(side * rows, rows), :],
+            frame_z[0, pl.ds(inward, rows), :],
+            horiz[c0, :],
+            diag[c0, :],
+            horiz[c1, :],
+        ]
+        for k, item in enumerate(items):
+            pack[k] = item
+            near_pack[k, own, :] = item
+            if k < 4:
+                wide[k] = jnp.zeros_like(wide[k])
+                wide[k, pl.ds(8, rows), :] = item
+        for to, first, second in ((0, rows - 1, rows - 2), (1, 0, 1)):
+            picks = [(0, first), (0, second), (1, first), (2, first), (3, first)]
+            for k, (item, row) in enumerate(picks):
+                mini_out[to, pl.ds(k, 1), :] = items[item][row : row + 1]
+            mini_out[to, pl.ds(5, 3), :] = jnp.zeros((3, levels), jnp.float32)
+
+    def send_frame(t, frame):
+        z = precondition(frame)
+        frame_z[t, pl.ds(0, z.shape[0]), :] = z
         if t == 0:
+            pl.when(border)(fill_packs)
             pl.semaphore_wait(barrier, n_all - 1)
 
-        @pl.when(border)
-        def _():
-            for j in sorted(range(n_gy), key=lambda j: abs(2 * j - n_gy)):
-                far_copy(t, lax.rem(gy + j, n_gy)).start()
-            if t < 2:
+            @pl.when(border)
+            def _():
+                for_rows(lambda side: mini_copy(side).start())
+
+        @pl.when(jnp.logical_not(east_border))
+        def _():
+            col_copy(t, 0).start()
+
+        @pl.when(jnp.logical_not(west_border))
+        def _():
+            col_copy(t, 1).start()
+
+        for_rows(lambda side: row_copy(t, side).start())
+        if t == 0:
+
+            @pl.when(border)
+            def _():
+                send_far(0)
                 for j in range(1, n_gy):
-                    near_copy(t, lax.rem(gy + j, n_gy)).start()
-
-        @pl.when(jnp.logical_not(east_border))
-        def _():
-            col_copy(t, 0).start()
-
-        @pl.when(jnp.logical_not(west_border))
-        def _():
-            col_copy(t, 1).start()
-
-    def send_rows(t):
-        @pl.when(has_north)
-        def _():
-            row_copy(t, 0).start()
-
-        @pl.when(has_south)
-        def _():
-            row_copy(t, 1).start()
+                    near_copy(lax.rem(gy + j, n_gy)).start()
+
+    def send_far(t):
+        for j in sorted(range(n_gy), key=lambda j: abs(2 * j - n_gy)):
+            far_copy(t, lax.rem(gy + j, n_gy)).start()
 
     def receive_rows(t):
         @pl.when(has_north)
@@ -315,37 +343,75 @@
 
     near_rest = pl.ds(0, (n_gy - 1) * rows)
 
-    def correct_first():
-        wait_bytes(far_pack, far_recv.at[0])
-        wait_bytes(near_pack.at[:, near_rest], near_recv.at[0])
+    def look_ahead():
+        c1 = edge_cols[1]
+        inner = pl.ds(8, rows)
+
+        def take(side, near, far):
+            mini_copy(side).wait_recv()
+            wide[0, pl.ds(near, 1), :] = mini_in[side, pl.ds(0, 1), :]
+            wide[0, pl.ds(far, 1), :] = mini_in[side, pl.ds(1, 1), :]
+            for k in (1, 2, 3):
+                wide[k, pl.ds(near, 1), :] = mini_in[side, pl.ds(k + 1, 1), :]
+
+        pl.when(border & has_south)(functools.partial(take, 0, 7, 6))
+        pl.when(border & has_north)(functools.partial(take, 1, 8 + rows, 9 + rows))
+
+        def next_to(w):
+            return pltpu.roll(w, w.shape[0] - 1, 0) + pltpu.roll(w, 1, 0)
+
+        z_edge, z_next, h_edge, d_edge = wide[0], wide[1], wide[2], wide[3]
+        v_edge = (
+            d_edge * z_edge
+            + h_edge * (4.0 * z_edge - z_next - next_to(z_edge))
+            + column_part(z_edge)
+        )
+        beside = next_to(z_next)[8 : 8 + rows] + z_edge[8 : 8 + rows]
+        z1 = z_next[8 : 8 + rows]
+        z2 = frame_z[0, pl.ds(2 * (rows + cols) + rows, rows), :]
+        v_next = (
+            diag[c1, :] * z1 + horiz[c1, :] * (4.0 * z1 - beside - z2) + column_part(z1)
+        )
+        z = precondition(jnp.concatenate([v_edge, v_next], 0))
+        z_edge, z_next = z[: rows + 16], z[rows + 16 :]
+        beside = next_to(z_edge)[8 : 8 + rows] + z_next
+        z_edge = z_edge[8 : 8 + rows]
+        h_own, d_own = h_edge[8 : 8 + rows], d_edge[8 : 8 + rows]
+        v = d_own * z_edge + h_own * (4.0 * z_edge - beside) + column_part(z_edge)
+        pack[5] = precondition(v)
+        pl.when(border)(functools.partial(send_far, 1))
+
+    def correct_early():
+        @pl.when(border)
+        def _():
+            wait_bytes(far_pack, far_recv.at[0])
+            wait_bytes(near_pack.at[:, near_rest], near_recv)
+
         gather_rows(0, tall, [(0, far_pack.at[0]), (1, near_pack.at[0])])
-        b_near = -(near_pack[1] * gathered[0])
-        b_far = -(far_pack[1] * gathered[1])
+        h_near, d_near = near_pack[2], near_pack[3]
+        h_far, d_far = far_pack[2], far_pack[3]
+        b_near, b_far = -(h_near * gathered[0]), -(h_far * gathered[1])
+        v_near = stencil(near_pack[0], d_near, h_near) - h_near * near_pack[1] + b_near
+        v_far = stencil(far_pack[0], d_far, h_far) - h_far * far_pack[1] + b_far
+        out = precondition(jnp.concatenate([b_near, v_near, b_far, v_far], 0), 2)
+        w_near, w_far = out[:tall, :levels], out[2 * tall : 3 * tall, levels:]
         strip[0] = b_near
-        both = precondition(jnp.concatenate([b_near, b_far], 0), 2)
-        strip[1] = both[:tall, :levels]
-        strip[2] = both[tall:, levels:]
-
-    def correct_second():
-        wait_bytes(far_z.at[0], far_recv.at[1])
-        wait_bytes(near_z.at[near_rest], near_recv.at[1])
-        w_near, w_far = strip[1], strip[2]
-        strip[3] = far_z[0] + w_far
-        strip[4] = near_z[...] + w_near
+        strip[1] = w_near
+        strip[3] = out[3 * tall :, levels:]
+        strip[4] = out[tall : 2 * tall, :levels]
         gather_rows(0, tall, [(0, strip.at[3]), (1, strip.at[4])])
-        h_near, h_far = near_pack[1], far_pack[1]
-        b_near = stencil(w_near, near_pack[2], h_near) - h_near * gathered[0]
-        b_far = stencil(w_far, far_pack[2], h_far) - h_far * gathered[1]
-        b_next = -(near_pack[3] * w_near)
-        all_three = precondition(jnp.concatenate([b_near, b_next, b_far], 0), 2)
-        w_edge, w_next = all_three[:tall, :levels], all_three[tall : 2 * tall, :levels]
+        b_near = stencil(w_near, d_near, h_near) - h_near * gathered[0]
+        b_far = stencil(w_far, d_far, h_far) - h_far * gathered[1]
+        b_next = -(near_pack[4] * w_near)
+        out = precondition(jnp.concatenate([b_near, b_next, b_far], 0), 2)
+        w_edge, w_next = out[:tall, :levels], out[tall : 2 * tall, :levels]
         strip[3] = b_near
         strip[4] = b_next
-        strip[5] = all_three[2 * tall :, levels:]
+        strip[5] = out[2 * tall :, levels:]
         strip[6] = w_edge
         strip[7] = w_next
         strip[8] = along(w_next)
-        strip[9] = stencil(w_edge, near_pack[2], h_near) - h_near * w_next
+        strip[9] = stencil(w_edge, d_near, h_near) - h_near * w_next
 
     def correct_third():
         c0, c1, c2 = edge_cols
@@ -354,8 +420,8 @@
         later = diag[c1, :] * w_next + h1 * (4.0 * w_next - beside - w_edge) + column_part(w_next)
         b_third = -(horiz[c2, :] * w_next)
         gather_rows(first_row, rows, [(2, strip.at[5])])
-        wait_bytes(far_z.at[1], far_recv.at[2])
-        gather_rows(first_row, rows, [(3, far_z.at[1])])
+        wait_bytes(far_last, far_recv.at[1])
+        gather_rows(first_row, rows, [(3, far_last)])
         across = gathered[2, pl.ds(0, rows), :] + gathered[3, pl.ds(0, rows), :]
         b_edge = strip[9, own, :] - horiz[c0, :] * across
         none = jnp.zeros((rows, levels), jnp.float32)
@@ -381,27 +447,32 @@
         load.wait()
     terms = {}
     spaces = [r0]
-    send_cols_on(0, edge_columns(r0))
+    frame = [edge_columns(r0), r0[south_edge, :], r0[north_edge, :]]
+    send_frame(0, jnp.concatenate(frame + [r0[c, :] for c in edge_cols[1:]], 0))
     edge_horiz = edge_columns(horiz)
     for t in range(ITERS):
         image = images.at[t]
         z = precondition(spaces[-1][...])
         fields[t] = z
-        send_rows(t)
         newest = len(spaces) - 1
         for i in range(len(spaces)):
             terms[(i, newest)] = product(spaces[i][...], spaces[newest][...])
         image[...] = inner_image(z)
+        if t == 0:
+            look_ahead()
+        if t == ITERS - 1:
+            correct_early()
         receive_rows(t)
         image[south_edge, :] = image[south_edge, :] - horiz[south_edge, :] * from_south[t]
         image[north_edge, :] = image[north_edge, :] - horiz[north_edge, :] * from_north[t]
         inside = edge_columns(image)
         receive_cols(t)
         edges = inside - edge_horiz * outside[...]
-        if t < ITERS - 1:
-            send_cols_on(t + 1, edges)
         image[east_edge, :] = edges[:rows]
         image[west_edge, :] = edges[rows:]
+        if t < ITERS - 1:
+            frame = [edges, image[south_edge, :], image[north_edge, :]]
+            send_frame(t + 1, jnp.concatenate(frame, 0))
         spaces.append(image)
     newest = len(spaces) - 1
     for i in range(len(spaces)):
@@ -411,8 +482,6 @@
 
     @pl.when(border)
     def _():
-        correct_first()
-        correct_second()
         correct_third()
 
     height = -(-len(KEYS) // 8) * 8
@@ -454,10 +523,9 @@
     @pl.when(border)
     def _():
         wait_bytes(far_pack, far_send.at[0])
-        wait_bytes(far_z.at[0], far_send.at[1])
-        wait_bytes(far_z.at[1], far_send.at[2])
-        wait_bytes(near_pack.at[:, near_rest], near_send.at[0])
-        wait_bytes(near_z.at[near_rest], near_send.at[1])
+        wait_bytes(far_last, far_send.at[1])
+        wait_bytes(near_pack.at[:, near_rest], near_send)
+        for_rows(lambda side: mini_copy(side).wait_send())
         c0, c1, c2 = edge_cols
         fields[1, c0, :] += strip[1, own, :]
         fields[2, c0, :] += strip[6, own, :]
@@ -525,15 +593,17 @@
             pltpu.VMEM(block, f32),
             pltpu.VMEM((1, levels), f32),
             pltpu.VMEM((2 * levels, levels), f32),
-            pltpu.VMEM((ITERS, 2 * rows, levels), f32),
+            pltpu.VMEM((ITERS, 4 * rows + 2 * cols, levels), f32),
             pltpu.VMEM((6, rows, levels), f32),
+            pltpu.VMEM((2, 8, levels), f32),
+            pltpu.VMEM((2, 8, levels), f32),
+            pltpu.VMEM((4, rows + 16, levels), f32),
             pltpu.VMEM((ITERS, rows, levels), f32),
             pltpu.VMEM((ITERS, rows, levels), f32),
             pltpu.VMEM((ITERS, cols, levels), f32),
             pltpu.VMEM((ITERS, cols, levels), f32),
-            pltpu.VMEM((3,) + column, f32),
             pltpu.VMEM((4,) + column, f32),
-            pltpu.VMEM((2,) + column, f32),
+            pltpu.VMEM((5,) + column, f32),
             pltpu.VMEM(column, f32),
             pltpu.VMEM((4,) + column, f32),
             pltpu.VMEM((10,) + column, f32),
@@ -545,8 +615,10 @@
             sems((ITERS, 2)),
             sems((ITERS,)),
             sems((ITERS,)),
-            sems((ITERS,)),
-            sems((ITERS,)),
+            sems((2,)),
+            sems((2,)),
+            sems(()),
+            sems(()),
             sems((2,)),
             sems((2,)),
             sems((ITERS, 2)),

time: 25.5 us -> 24.7 us (0.969)
  Pallas kernels: 24.7 us -> 23.9 us
    pallas_call x1, Pallas kernels: 22.8 us -> 21.9 us  [on_device(): pl.pallas_call(functools.partial(kernel, n_gx, n_gy, rows), out_shape=(ba...]
where the time goes in v2:
time: 24.7 us; the launch traced here: 24.5 us
  Pallas kernels  23.9 us (97%)
  between operations  0.64 us (3%)
    pallas_call x1, Pallas kernels, on_device(): pl.pallas_call(functools.partial(kernel, n_gx, n_gy, rows), out_shape=(ba...  21.9 us
    pallas_call x1, Pallas kernels, on_device(): pl.pallas_call(functools.partial(finish, total_cells), out_shape=(jax.Sha...  1.96 us

profile of v2, /device:TPU:0, one launch (start us, length us, event | category | flops | bytes accessed | tf_op | source)
XLA Modules:
  0.0 24.5 jit_solution(9378780141405717569)
XLA Ops:
  0.6 21.9 %shard_map.85 = (f32[3,256,128]{2,1,0:T(8,128)S(1)}, f32[3,256,128]{2,1,0:T(8,128)S(1)}, f32[1,128]{1,0:T(1,128)S(1)}, f32[256,128]{1,0:T(8,128)S(1)}) custom-call(s32[2,64]{1,0:T(2,128)} %edge_table.1, f32[256,128]{1,0:T(8,128)} %bitcast.7, f32[256,128]{1,0:T(8,128)} %bitcast.8, f32[256,128]{1,0:T(8,128)} %bitcast.9, f32[1,128]{1,0:T(1,128)} %bitcast.10, ...), custom_call_target="tpu_custom_call" | custom-call | tf_op jit(solution)/shard_map/pallas_call | solution.py:586
  22.6 2.0 %shard_map.86 = (f32[256,128]{1,0:T(8,128)}, f32[256,128]{1,0:T(8,128)}, f32[1,3]{1,0:T(1,128)}) custom-call(f32[1,128]{1,0:T(1,128)S(1)} %get-tuple-element.10.all_totals, f32[256,128]{1,0:T(8,128)S(1)} %get-tuple-element.11.r0, f32[3,256,128]{2,1,0:T(8,128)S(1)} %get-tuple-element.12.fields, f32[3,256,128]{2,1,0:T(8,128)S(1)} %get-tuple-element.13.images), custom_call_target="tpu_custom_call" | custom-call | tf_op jit(solution)/shard_map/pallas_call | solution.py:643

commit v3 on v2

--- a/solution.py
+++ b/solution.py
@@ -56,6 +56,8 @@
     west_recv,
     far_send,
     far_recv,
+    relay_send,
+    relay_recv,
     near_send,
     near_recv,
     mini_send,
@@ -162,6 +164,16 @@
             send_sem=far_send.at[t],
             recv_sem=far_recv.at[t],
             device_id=(far_x, g),
+            device_id_type=MESH,
+        )
+
+    def relay_copy(g):
+        return pltpu.make_async_remote_copy(
+            src_ref=far_pack.at[:, own],
+            dst_ref=far_pack.at[:, own],
+            send_sem=relay_send,
+            recv_sem=relay_recv,
+            device_id=(gx, g),
             device_id_type=MESH,
         )
 
@@ -255,12 +267,13 @@
 
             @pl.when(border)
             def _():
-                send_far(0)
+                far_copy(0, gy).start()
+                pl.when(gx == 0)(functools.partial(send_far, 0, 1))
                 for j in range(1, n_gy):
                     near_copy(lax.rem(gy + j, n_gy)).start()
 
-    def send_far(t):
-        for j in sorted(range(n_gy), key=lambda j: abs(2 * j - n_gy)):
+    def send_far(t, first=0):
+        for j in sorted(range(first, n_gy), key=lambda j: abs(2 * j - n_gy)):
             far_copy(t, lax.rem(gy + j, n_gy)).start()
 
     def receive_rows(t):
@@ -342,6 +355,14 @@
         pltpu.make_async_copy(ref, ref, sem).wait()
 
     near_rest = pl.ds(0, (n_gy - 1) * rows)
+    last = gx == n_gx - 1
+    relays = border & jnp.logical_not(last)
+
+    def relay():
+        wait_bytes(far_pack.at[:, own], far_recv.at[0])
+        for j in sorted(range(1, n_gy), key=lambda j: abs(2 * j - n_gy)):
+            relay_copy(lax.rem(gy + j, n_gy)).start()
+
 
     def look_ahead():
         c1 = edge_cols[1]
@@ -384,7 +405,8 @@
     def correct_early():
         @pl.when(border)
         def _():
-            wait_bytes(far_pack, far_recv.at[0])
+            pl.when(last)(lambda: wait_bytes(far_pack, far_recv.at[0]))
+            pl.when(relays)(lambda: wait_bytes(far_pack.at[:, near_rest], relay_recv))
             wait_bytes(near_pack.at[:, near_rest], near_recv)
 
         gather_rows(0, tall, [(0, far_pack.at[0]), (1, near_pack.at[0])])
@@ -460,6 +482,8 @@
         image[...] = inner_image(z)
         if t == 0:
             look_ahead()
+        if t == 1:
+            pl.when(relays)(relay)
         if t == ITERS - 1:
             correct_early()
         receive_rows(t)
@@ -522,7 +546,9 @@
 
     @pl.when(border)
     def _():
-        wait_bytes(far_pack, far_send.at[0])
+        wait_bytes(far_pack.at[:, own], far_send.at[0])
+        pl.when(gx == 0)(lambda: wait_bytes(far_pack.at[:, near_rest], far_send.at[0]))
+        pl.when(relays)(lambda: wait_bytes(far_pack.at[:, near_rest], relay_send))
         wait_bytes(far_last, far_send.at[1])
         wait_bytes(near_pack.at[:, near_rest], near_send)
         for_rows(lambda side: mini_copy(side).wait_send())
@@ -619,6 +645,8 @@
             sems((2,)),
             sems(()),
             sems(()),
+            sems(()),
+            sems(()),
             sems((2,)),
             sems((2,)),
             sems((ITERS, 2)),

time: 24.7 us -> 22.7 us (0.919)
  Pallas kernels: 23.9 us -> 21.9 us
    pallas_call x1, Pallas kernels: 21.9 us -> 20 us  [on_device(): pl.pallas_call(functools.partial(kernel, n_gx, n_gy, rows), out_shape=(ba...]
where the time goes in v3:
time: 22.7 us; the launch traced here: 22.6 us
  Pallas kernels  21.9 us (96%)
  between operations  0.64 us (3%)
    pallas_call x1, Pallas kernels, on_device(): pl.pallas_call(functools.partial(kernel, n_gx, n_gy, rows), out_shape=(ba...  20 us
    pallas_call x1, Pallas kernels, on_device(): pl.pallas_call(functools.partial(finish, total_cells), out_shape=(jax.Sha...  1.96 us

profile of v3, /device:TPU:0, one launch (start us, length us, event | category | flops | bytes accessed | tf_op | source)
XLA Modules:
  0.0 22.6 jit_solution(3318828583511115943)
XLA Ops:
  0.6 20.0 %shard_map.85 = (f32[3,256,128]{2,1,0:T(8,128)S(1)}, f32[3,256,128]{2,1,0:T(8,128)S(1)}, f32[1,128]{1,0:T(1,128)S(1)}, f32[256,128]{1,0:T(8,128)S(1)}) custom-call(s32[2,64]{1,0:T(2,128)} %edge_table.1, f32[256,128]{1,0:T(8,128)} %bitcast.7, f32[256,128]{1,0:T(8,128)} %bitcast.8, f32[256,128]{1,0:T(8,128)} %bitcast.9, f32[1,128]{1,0:T(1,128)} %bitcast.10, ...), custom_call_target="tpu_custom_call" | custom-call | tf_op jit(solution)/shard_map/pallas_call | solution.py:612
  20.6 2.0 %shard_map.86 = (f32[256,128]{1,0:T(8,128)}, f32[256,128]{1,0:T(8,128)}, f32[1,3]{1,0:T(1,128)}) custom-call(f32[1,128]{1,0:T(1,128)S(1)} %get-tuple-element.10.all_totals, f32[256,128]{1,0:T(8,128)S(1)} %get-tuple-element.11.r0, f32[3,256,128]{2,1,0:T(8,128)S(1)} %get-tuple-element.12.fields, f32[3,256,128]{2,1,0:T(8,128)S(1)} %get-tuple-element.13.images), custom_call_target="tpu_custom_call" | custom-call | tf_op jit(solution)/shard_map/pallas_call | solution.py:671

commit v4 on v3

--- a/solution.py
+++ b/solution.py
@@ -32,6 +32,7 @@
     horiz,
     vert,
     matrix,
+    weights,
     frame_z,
     pack,
     mini_out,
@@ -135,14 +136,26 @@
 
     outside[...] = jnp.zeros_like(outside)
 
-    def precondition(v, panels=1):
-        return lax.dot_general(
-            v,
-            matrix[pl.ds(0, panels * levels), :],
+    def split(v):
+        high = v.astype(jnp.bfloat16)
+        return high, (v - high.astype(jnp.float32)).astype(jnp.bfloat16)
+
+    def prepare_weights():
+        for which in range(2):
+            for part, value in enumerate(split(matrix[pl.ds(which * levels, levels), :])):
+                for twice in range(2):
+                    weights[
+                        which, pl.ds(part * levels, levels), pl.ds(twice * levels, levels)
+                    ] = value
+
+    def precondition(v, which=0):
+        out = lax.dot_general(
+            jnp.concatenate(split(v), 1),
+            weights[which],
             (((1,), (1,)), ((), ())),
-            precision=lax.Precision.HIGHEST,
             preferred_element_type=jnp.float32,
         )
+        return out[:, :levels] + out[:, levels:]
 
     def col_copy(t, side):
         buffer, recv, x = (
@@ -415,21 +428,22 @@
         b_near, b_far = -(h_near * gathered[0]), -(h_far * gathered[1])
         v_near = stencil(near_pack[0], d_near, h_near) - h_near * near_pack[1] + b_near
         v_far = stencil(far_pack[0], d_far, h_far) - h_far * far_pack[1] + b_far
-        out = precondition(jnp.concatenate([b_near, v_near, b_far, v_far], 0), 2)
-        w_near, w_far = out[:tall, :levels], out[2 * tall : 3 * tall, levels:]
+        near = precondition(jnp.concatenate([b_near, v_near], 0))
+        far = precondition(jnp.concatenate([b_far, v_far], 0), 1)
+        w_near, w_far = near[:tall], far[:tall]
         strip[0] = b_near
         strip[1] = w_near
-        strip[3] = out[3 * tall :, levels:]
-        strip[4] = out[tall : 2 * tall, :levels]
+        strip[3] = far[tall:]
+        strip[4] = near[tall:]
         gather_rows(0, tall, [(0, strip.at[3]), (1, strip.at[4])])
         b_near = stencil(w_near, d_near, h_near) - h_near * gathered[0]
         b_far = stencil(w_far, d_far, h_far) - h_far * gathered[1]
         b_next = -(near_pack[4] * w_near)
-        out = precondition(jnp.concatenate([b_near, b_next, b_far], 0), 2)
-        w_edge, w_next = out[:tall, :levels], out[tall : 2 * tall, :levels]
+        near = precondition(jnp.concatenate([b_near, b_next], 0))
+        w_edge, w_next = near[:tall], near[tall:]
         strip[3] = b_near
         strip[4] = b_next
-        strip[5] = out[2 * tall :, levels:]
+        strip[5] = precondition(b_far, 1)
         strip[6] = w_edge
         strip[7] = w_next
         strip[8] = along(w_next)
@@ -467,6 +481,7 @@
 
     for load in loads:
         load.wait()
+    prepare_weights()
     terms = {}
     spaces = [r0]
     frame = [edge_columns(r0), r0[south_edge, :], r0[north_edge, :]]
@@ -619,6 +634,7 @@
             pltpu.VMEM(block, f32),
             pltpu.VMEM((1, levels), f32),
             pltpu.VMEM((2 * levels, levels), f32),
+            pltpu.VMEM((2, 2 * levels, 2 * levels), jnp.bfloat16),
             pltpu.VMEM((ITERS, 4 * rows + 2 * cols, levels), f32),
             pltpu.VMEM((6, rows, levels), f32),
             pltpu.VMEM((2, 8, levels), f32),

time: 22.7 us -> 22.5 us (level)
    pallas_call x1, Pallas kernels: 20 us -> 19.7 us  [on_device(): pl.pallas_call(functools.partial(kernel, n_gx, n_gy, rows), out_shape=(ba...]
where the time goes in v4:
time: 22.5 us; the launch traced here: 22.3 us
  Pallas kernels  21.7 us (96%)
  between operations  0.64 us (3%)
    pallas_call x1, Pallas kernels, on_device(): pl.pallas_call(functools.partial(kernel, n_gx, n_gy, rows), out_shape=(ba...  19.7 us
    pallas_call x1, Pallas kernels, on_device(): pl.pallas_call(functools.partial(finish, total_cells), out_shape=(jax.Sha...  1.96 us

profile of v4, /device:TPU:0, one launch (start us, length us, event | category | flops | bytes accessed | tf_op | source)
XLA Modules:
  0.0 22.3 jit_solution(15202255945354177516)
XLA Ops:
  0.6 19.7 %shard_map.85 = (f32[3,256,128]{2,1,0:T(8,128)S(1)}, f32[3,256,128]{2,1,0:T(8,128)S(1)}, f32[1,128]{1,0:T(1,128)S(1)}, f32[256,128]{1,0:T(8,128)S(1)}) custom-call(s32[2,64]{1,0:T(2,128)} %edge_table.1, f32[256,128]{1,0:T(8,128)} %bitcast.7, f32[256,128]{1,0:T(8,128)} %bitcast.8, f32[256,128]{1,0:T(8,128)} %bitcast.9, f32[1,128]{1,0:T(1,128)} %bitcast.10, ...), custom_call_target="tpu_custom_call" | custom-call | tf_op jit(solution)/shard_map/pallas_call | solution.py:627
  20.4 2.0 %shard_map.86 = (f32[256,128]{1,0:T(8,128)}, f32[256,128]{1,0:T(8,128)}, f32[1,3]{1,0:T(1,128)}) custom-call(f32[1,128]{1,0:T(1,128)S(1)} %get-tuple-element.10.all_totals, f32[256,128]{1,0:T(8,128)S(1)} %get-tuple-element.11.r0, f32[3,256,128]{2,1,0:T(8,128)S(1)} %get-tuple-element.12.fields, f32[3,256,128]{2,1,0:T(8,128)S(1)} %get-tuple-element.13.images), custom_call_target="tpu_custom_call" | custom-call | tf_op jit(solution)/shard_map/pallas_call | solution.py:687

commit v5 on v4

--- a/solution.py
+++ b/solution.py
@@ -578,10 +578,14 @@
     wait_bytes(others, sum_send)
 
 
-def finish(total_cells, all_totals, r0, fields, images, out_x, out_r, out_norms, x, r, sem):
+def finish(
+    total_cells, all_totals, r0, fields, images, out_x, out_r, out_norms, x, r, norms_out, sem, norm_sem
+):
     levels = r0.shape[-1]
     totals = all_totals[...]
-    value = {key: totals[:, k : k + 1] for k, key in enumerate(KEYS)}
+    value = {
+        key: jnp.broadcast_to(totals[:, k : k + 1], (8, levels)) for k, key in enumerate(KEYS)
+    }
 
     rho, g0, g1, g2 = value[(0, 0)], value[(0, 1)], value[(0, 2)], value[(0, 3)]
     a00, a01, a02 = value[(1, 1)], value[(1, 2)], value[(1, 3)]
@@ -596,13 +600,15 @@
     norm2 = norm1 - y2 * f2
     y1 = y1 - l21 * y2
     y0 = y0 - l10 * y1 - l20 * y2
-    norm_lane = lax.broadcasted_iota(jnp.int32, (1, levels), 1)
+    norm_lane = lax.broadcasted_iota(jnp.int32, (8, levels), 1)
     norms = jnp.where(norm_lane == 0, norm0, jnp.where(norm_lane == 1, norm1, norm2))
-    out_norms[...] = norms[:, :ITERS] / total_cells
+    norms_out[...] = norms[:1, :ITERS] / total_cells
+    copies = [pltpu.make_async_copy(norms_out, out_norms, norm_sem)]
+    copies[0].start()
     rows = r0.shape[0]
     pieces = 2 if rows % 16 == 0 else 1
     size = rows // pieces
-    copies = []
+    y0, y1, y2 = (jnp.tile(y, (size // 8, 1)) for y in (y0, y1, y2))
     for p in range(pieces):
         span = pl.ds(p * size, size)
         x[span] = y0 * fields[0, span] + y1 * fields[1, span] + y2 * fields[2, span]
@@ -692,8 +698,14 @@
             jax.ShapeDtypeStruct((1, ITERS), f32),
         ),
         in_specs=[VMEM, VMEM, VMEM, VMEM],
-        out_specs=(ANY, ANY, VMEM),
-        scratch_shapes=[pltpu.VMEM(block, f32), pltpu.VMEM(block, f32), sems((2, 2))],
+        out_specs=(ANY, ANY, ANY),
+        scratch_shapes=[
+            pltpu.VMEM(block, f32),
+            pltpu.VMEM(block, f32),
+            pltpu.VMEM((1, ITERS), f32),
+            sems((2, 2)),
+            sems(()),
+        ],
     )(in_vmem(totals), in_vmem(start), in_vmem(fields), in_vmem(images))
     shape = right_side.shape
     return x.reshape(shape), r.reshape(shape), norms.reshape(ITERS)

time: 22.5 us -> 21.4 us (0.951)
  Pallas kernels: 21.7 us -> 20.6 us
    pallas_call x1, Pallas kernels: 1.96 us -> 0.86 us  [on_device(): pl.pallas_call(functools.partial(finish, total_cells), out_shape=(jax.Sha...]
where the time goes in v5:
time: 21.4 us; the launch traced here: 21.2 us
  Pallas kernels  20.6 us (96%)
  between operations  0.64 us (3%)
    pallas_call x1, Pallas kernels, on_device(): pl.pallas_call(functools.partial(kernel, n_gx, n_gy, rows), out_shape=(ba...  19.7 us
    pallas_call x1, Pallas kernels, on_device(): pl.pallas_call(functools.partial(finish, total_cells), out_shape=(jax.Sha...  0.86 us

profile of v5, /device:TPU:0, one launch (start us, length us, event | category | flops | bytes accessed | tf_op | source)
XLA Modules:
  0.0 21.2 jit_solution(11222663133584522538)
XLA Ops:
  0.6 19.7 %shard_map.85 = (f32[3,256,128]{2,1,0:T(8,128)S(1)}, f32[3,256,128]{2,1,0:T(8,128)S(1)}, f32[1,128]{1,0:T(1,128)S(1)}, f32[256,128]{1,0:T(8,128)S(1)}) custom-call(s32[2,64]{1,0:T(2,128)} %edge_table.1, f32[256,128]{1,0:T(8,128)} %bitcast.7, f32[256,128]{1,0:T(8,128)} %bitcast.8, f32[256,128]{1,0:T(8,128)} %bitcast.9, f32[1,128]{1,0:T(1,128)} %bitcast.10, ...), custom_call_target="tpu_custom_call" | custom-call | tf_op jit(solution)/shard_map/pallas_call | solution.py:633
  20.4 0.9 %shard_map.86 = (f32[256,128]{1,0:T(8,128)}, f32[256,128]{1,0:T(8,128)}, f32[1,3]{1,0:T(1,128)}) custom-call(f32[1,128]{1,0:T(1,128)S(1)} %get-tuple-element.10.all_totals, f32[256,128]{1,0:T(8,128)S(1)} %get-tuple-element.11.r0, f32[3,256,128]{2,1,0:T(8,128)S(1)} %get-tuple-element.12.fields, f32[3,256,128]{2,1,0:T(8,128)S(1)} %get-tuple-element.13.images), custom_call_target="tpu_custom_call" | custom-call | tf_op jit(solution)/shard_map/pallas_call | solution.py:693

commit v6 on v5

--- a/solution.py
+++ b/solution.py
@@ -38,6 +38,11 @@
     mini_out,
     mini_in,
     wide,
+    edge_out,
+    edge_in,
+    corner_out,
+    corner_in,
+    beyond,
     from_east,
     from_west,
     from_north,
@@ -47,6 +52,7 @@
     far_last,
     gathered,
     strip,
+    strip_out,
     outside,
     partial,
     sums,
@@ -63,6 +69,10 @@
     near_recv,
     mini_send,
     mini_recv,
+    edge_send,
+    edge_recv,
+    corner_send,
+    corner_recv,
     row_send,
     north_recv,
     south_recv,
@@ -180,10 +190,10 @@
             device_id_type=MESH,
         )
 
-    def relay_copy(g):
+    def relay_copy(g, block):
         return pltpu.make_async_remote_copy(
-            src_ref=far_pack.at[:, own],
-            dst_ref=far_pack.at[:, own],
+            src_ref=far_pack.at[:, block],
+            dst_ref=far_pack.at[:, block],
             send_sem=relay_send,
             recv_sem=relay_recv,
             device_id=(gx, g),
@@ -225,6 +235,37 @@
             device_id_type=MESH,
         )
 
+    def edge_copy(side):
+        return pltpu.make_async_remote_copy(
+            src_ref=edge_out.at[side],
+            dst_ref=edge_in.at[1 - side],
+            send_sem=edge_send.at[side],
+            recv_sem=edge_recv.at[1 - side],
+            device_id=(east_x if side == 0 else west_x, gy),
+            device_id_type=MESH,
+        )
+
+    def corner_copy(k):
+        return pltpu.make_async_remote_copy(
+            src_ref=corner_out.at[k],
+            dst_ref=corner_in.at[k],
+            send_sem=corner_send.at[k],
+            recv_sem=corner_recv.at[k],
+            device_id=(west_x if k < 2 else east_x, gy + 1 if k % 2 == 0 else gy - 1),
+            device_id_type=MESH,
+        )
+
+    def for_sides(visit):
+        pl.when(jnp.logical_not(east_border))(functools.partial(visit, 0))
+        pl.when(jnp.logical_not(west_border))(functools.partial(visit, 1))
+
+    def for_corners(visit, sending):
+        for k in range(4):
+            east = (k < 2) != sending
+            north = (k % 2 == 0) == sending
+            condition = jnp.logical_not(east_border if east else west_border)
+            pl.when(condition & (has_north if north else has_south))(functools.partial(visit, k))
+
     def for_rows(visit):
         @pl.when(has_north)
         def _():
@@ -234,12 +275,39 @@
         def _():
             visit(1)
 
+    inward = 2 * (rows + cols)
+    mid = pl.ds(8, rows)
+
+    def side_cols(side, k):
+        return pl.ds(k if side else cols - 1 - k, rows, stride=cols)
+
+    def fill_edges():
+        for side in range(2):
+            items = [
+                frame_z[0, pl.ds(side * rows, rows), :],
+                frame_z[0, pl.ds(inward + side * rows, rows), :],
+                horiz[side_cols(side, 0), :],
+                diag[side_cols(side, 0), :],
+            ]
+            for k, item in enumerate(items):
+                wide[side, k] = jnp.zeros_like(wide[side, k])
+                wide[side, k, mid, :] = item
+                if k:
+                    edge_out[side, k - 1] = item
+            for to, first, second in ((0, rows - 1, rows - 2), (1, 0, 1)):
+                picks = [(0, first), (0, second), (1, first), (2, first), (3, first)]
+                for k, (item, row) in enumerate(picks):
+                    mini_out[to, pl.ds(8 * side + k, 1), :] = items[item][row : row + 1]
+                mini_out[to, pl.ds(8 * side + 5, 3), :] = jnp.zeros((3, levels), jnp.float32)
+                corner_out[2 * (1 - side) + to] = jnp.zeros((8, levels), jnp.float32)
+                corner_out[2 * (1 - side) + to, pl.ds(0, 1), :] = items[0][first : first + 1]
+        beyond[...] = jnp.zeros_like(beyond)
+
     def fill_packs():
         c0, c1, c2 = edge_cols
-        inward = 2 * (rows + cols)
         items = [
             frame_z[0, pl.ds(side * rows, rows), :],
-            frame_z[0, pl.ds(inward, rows), :],
+            frame_z[0, pl.ds(inward + side * rows, rows), :],
             horiz[c0, :],
             diag[c0, :],
             horiz[c1, :],
@@ -247,47 +315,37 @@
         for k, item in enumerate(items):
             pack[k] = item
             near_pack[k, own, :] = item
-            if k < 4:
-                wide[k] = jnp.zeros_like(wide[k])
-                wide[k, pl.ds(8, rows), :] = item
-        for to, first, second in ((0, rows - 1, rows - 2), (1, 0, 1)):
-            picks = [(0, first), (0, second), (1, first), (2, first), (3, first)]
-            for k, (item, row) in enumerate(picks):
-                mini_out[to, pl.ds(k, 1), :] = items[item][row : row + 1]
-            mini_out[to, pl.ds(5, 3), :] = jnp.zeros((3, levels), jnp.float32)
-
-    def send_frame(t, frame):
-        z = precondition(frame)
-        frame_z[t, pl.ds(0, z.shape[0]), :] = z
-        if t == 0:
-            pl.when(border)(fill_packs)
-            pl.semaphore_wait(barrier, n_all - 1)
-
-            @pl.when(border)
-            def _():
-                for_rows(lambda side: mini_copy(side).start())
-
-        @pl.when(jnp.logical_not(east_border))
+
+    def send_first(frame):
+        frame_z[0] = precondition(frame)
+        fill_edges()
+        pl.when(border)(fill_packs)
+        pl.semaphore_wait(barrier, n_all - 1)
+
+        @pl.when(gx == 0)
         def _():
-            col_copy(t, 0).start()
-
-        @pl.when(jnp.logical_not(west_border))
+            for j in range(0, n_gy, 2):
+                far_copy(0, lax.rem(gy + j, n_gy)).start()
+
+        for_sides(lambda side: col_copy(0, side).start())
+        for_rows(lambda side: mini_copy(side).start())
+        for_rows(lambda side: row_copy(0, side).start())
+        for_corners(lambda k: corner_copy(k).start(), True)
+        for_sides(lambda side: edge_copy(side).start())
+
+        @pl.when(border)
         def _():
-            col_copy(t, 1).start()
-
+            pl.when(gx > 0)(lambda: far_copy(0, gy).start())
+            for j in range(1, n_gy):
+                near_copy(lax.rem(gy + j, n_gy)).start()
+
+    def send_rows(t, frame):
+        frame_z[t, pl.ds(2 * rows, 2 * cols), :] = precondition(frame)
         for_rows(lambda side: row_copy(t, side).start())
-        if t == 0:
-
-            @pl.when(border)
-            def _():
-                far_copy(0, gy).start()
-                pl.when(gx == 0)(functools.partial(send_far, 0, 1))
-                for j in range(1, n_gy):
-                    near_copy(lax.rem(gy + j, n_gy)).start()
-
-    def send_far(t, first=0):
-        for j in sorted(range(first, n_gy), key=lambda j: abs(2 * j - n_gy)):
-            far_copy(t, lax.rem(gy + j, n_gy)).start()
+
+    def send_far_last():
+        for j in sorted(range(n_gy), key=lambda j: abs(2 * j - n_gy)):
+            far_copy(1, lax.rem(gy + j, n_gy)).start()
 
     def receive_rows(t):
         @pl.when(has_north)
@@ -299,15 +357,14 @@
             row_copy(t, 0).wait_recv()
 
     def receive_cols(t):
-        @pl.when(jnp.logical_not(east_border))
-        def _():
-            col_copy(t, 1).wait_recv()
-            outside[pl.ds(0, rows), :] = from_east[t]
-
-        @pl.when(jnp.logical_not(west_border))
-        def _():
-            col_copy(t, 0).wait_recv()
-            outside[pl.ds(rows, rows), :] = from_west[t]
+        def take(side):
+            buffer = from_west if side else from_east
+            col_copy(t, 1 - side).wait_recv()
+            outside[pl.ds(side * rows, rows), :] = buffer[t]
+            if t == 0:
+                beyond[side, mid, :] = buffer[t]
+
+        for_sides(take)
 
     col_id = lax.rem(lax.broadcasted_iota(jnp.int32, (cells, levels), 0), cols)
     east_edge = pl.ds(cols - 1, rows, stride=cols)
@@ -370,31 +427,43 @@
     near_rest = pl.ds(0, (n_gy - 1) * rows)
     last = gx == n_gx - 1
     relays = border & jnp.logical_not(last)
+    alike = pl.ds(0, n_gy // 2 * rows)
+
+    def relay_across():
+        wait_bytes(far_pack.at[:, alike], far_recv.at[0])
+        for k in range(n_gy // 2):
+            g = lax.rem(gy, 2) + 2 * k
+            block = pl.ds(pl.multiple_of(g * rows, rows), rows)
+            relay_copy(gy + 1 - 2 * lax.rem(gy, 2), block).start()
 
     def relay():
         wait_bytes(far_pack.at[:, own], far_recv.at[0])
         for j in sorted(range(1, n_gy), key=lambda j: abs(2 * j - n_gy)):
-            relay_copy(lax.rem(gy + j, n_gy)).start()
-
+            relay_copy(lax.rem(gy + j, n_gy), own).start()
+
+
+    def next_to(w):
+        return pltpu.roll(w, w.shape[0] - 1, 0) + pltpu.roll(w, 1, 0)
+
+    def strip_image(side, k, z, left, right):
+        c = side_cols(side, k)
+        return diag[c, :] * z + horiz[c, :] * (4.0 * z - left - right) + column_part(z)
 
     def look_ahead():
         c1 = edge_cols[1]
-        inner = pl.ds(8, rows)
-
-        def take(side, near, far):
-            mini_copy(side).wait_recv()
-            wide[0, pl.ds(near, 1), :] = mini_in[side, pl.ds(0, 1), :]
-            wide[0, pl.ds(far, 1), :] = mini_in[side, pl.ds(1, 1), :]
-            for k in (1, 2, 3):
-                wide[k, pl.ds(near, 1), :] = mini_in[side, pl.ds(k + 1, 1), :]
-
-        pl.when(border & has_south)(functools.partial(take, 0, 7, 6))
-        pl.when(border & has_north)(functools.partial(take, 1, 8 + rows, 9 + rows))
-
-        def next_to(w):
-            return pltpu.roll(w, w.shape[0] - 1, 0) + pltpu.roll(w, 1, 0)
-
-        z_edge, z_next, h_edge, d_edge = wide[0], wide[1], wide[2], wide[3]
+
+        def take(direction, near, far):
+            mini_copy(direction).wait_recv()
+            for side in range(2):
+                row = mini_in.at[direction]
+                wide[side, 0, pl.ds(near, 1), :] = row[pl.ds(8 * side, 1), :]
+                wide[side, 0, pl.ds(far, 1), :] = row[pl.ds(8 * side + 1, 1), :]
+                for k in (1, 2, 3):
+                    wide[side, k, pl.ds(near, 1), :] = row[pl.ds(8 * side + k + 1, 1), :]
+
+        pl.when(has_south)(functools.partial(take, 0, 7, 6))
+        pl.when(has_north)(functools.partial(take, 1, 8 + rows, 9 + rows))
+        z_edge, z_next, h_edge, d_edge = (wide[side, k] for k in range(4))
         v_edge = (
             d_edge * z_edge
             + h_edge * (4.0 * z_edge - z_next - next_to(z_edge))
@@ -402,7 +471,7 @@
         )
         beside = next_to(z_next)[8 : 8 + rows] + z_edge[8 : 8 + rows]
         z1 = z_next[8 : 8 + rows]
-        z2 = frame_z[0, pl.ds(2 * (rows + cols) + rows, rows), :]
+        z2 = frame_z[0, pl.ds(inward + (2 + side) * rows, rows), :]
         v_next = (
             diag[c1, :] * z1 + horiz[c1, :] * (4.0 * z1 - beside - z2) + column_part(z1)
         )
@@ -413,12 +482,58 @@
         h_own, d_own = h_edge[8 : 8 + rows], d_edge[8 : 8 + rows]
         v = d_own * z_edge + h_own * (4.0 * z_edge - beside) + column_part(z_edge)
         pack[5] = precondition(v)
-        pl.when(border)(functools.partial(send_far, 1))
+        pl.when(border)(send_far_last)
+
+    def look_across():
+        for_sides(lambda side: edge_copy(1 - side).wait_recv())
+
+        def take(k):
+            corner_copy(k).wait_recv()
+            row = 8 + rows if k % 2 else 7
+            beyond[k // 2, pl.ds(row, 1), :] = corner_in[k, pl.ds(0, 1), :]
+
+        for_corners(take, False)
+        images_first = []
+        for side in range(2):
+            z_edge, z_next, h_edge, d_edge = (wide[side, k] for k in range(4))
+            z_out = beyond[side]
+            own_edge, own_out = z_edge[8 : 8 + rows], z_out[8 : 8 + rows]
+            v_edge = (
+                d_edge * z_edge
+                + h_edge * (4.0 * z_edge - z_next - z_out - next_to(z_edge))
+                + column_part(z_edge)
+            )
+            z1 = z_next[8 : 8 + rows]
+            z2 = frame_z[0, pl.ds(inward + (2 + side) * rows, rows), :]
+            v_next = strip_image(side, 1, z1, next_to(z_next)[8 : 8 + rows] + own_edge, z2)
+            v_out = (
+                edge_in[side, 2] * own_out
+                + edge_in[side, 1]
+                * (4.0 * own_out - edge_in[side, 0] - own_edge - next_to(z_out)[8 : 8 + rows])
+                + column_part(own_out)
+            )
+            images_first += [v_edge, v_next, v_out]
+        z = precondition(jnp.concatenate(images_first, 0))
+        second = []
+        each = 3 * rows + 16
+        for side in range(2):
+            part = z[side * each : (side + 1) * each]
+            z_edge, z_next, z_out = part[: rows + 16], part[rows + 16 : each - rows], part[each - rows :]
+            strip_out[pl.ds(side * rows, rows), :] = z_out
+            beside = next_to(z_edge)[8 : 8 + rows]
+            second.append(strip_image(side, 0, z_edge[8 : 8 + rows], beside + z_next, z_out))
+        frame_z[2, pl.ds(0, 2 * rows), :] = precondition(jnp.concatenate(second, 0))
+
+        def give(side):
+            col_copy(2, side).start()
+            outside[pl.ds(side * rows, rows), :] = strip_out[pl.ds(side * rows, rows), :]
+
+        for_sides(give)
 
     def correct_early():
         @pl.when(border)
         def _():
-            pl.when(last)(lambda: wait_bytes(far_pack, far_recv.at[0]))
+            pl.when(last)(lambda: wait_bytes(far_pack.at[:, alike], relay_recv))
             pl.when(relays)(lambda: wait_bytes(far_pack.at[:, near_rest], relay_recv))
             wait_bytes(near_pack.at[:, near_rest], near_recv)
 
@@ -485,7 +600,8 @@
     terms = {}
     spaces = [r0]
     frame = [edge_columns(r0), r0[south_edge, :], r0[north_edge, :]]
-    send_frame(0, jnp.concatenate(frame + [r0[c, :] for c in edge_cols[1:]], 0))
+    frame += [r0[side_cols(side, k), :] for k in (1, 2) for side in range(2)]
+    send_first(jnp.concatenate(frame, 0))
     edge_horiz = edge_columns(horiz)
     for t in range(ITERS):
         image = images.at[t]
@@ -499,19 +615,21 @@
             look_ahead()
         if t == 1:
             pl.when(relays)(relay)
-        if t == ITERS - 1:
+            look_across()
+        if t == 2:
+            pl.when(last)(relay_across)
             correct_early()
         receive_rows(t)
         image[south_edge, :] = image[south_edge, :] - horiz[south_edge, :] * from_south[t]
         image[north_edge, :] = image[north_edge, :] - horiz[north_edge, :] * from_north[t]
         inside = edge_columns(image)
-        receive_cols(t)
+        if t != 1:
+            receive_cols(t)
         edges = inside - edge_horiz * outside[...]
         image[east_edge, :] = edges[:rows]
         image[west_edge, :] = edges[rows:]
         if t < ITERS - 1:
-            frame = [edges, image[south_edge, :], image[north_edge, :]]
-            send_frame(t + 1, jnp.concatenate(frame, 0))
+            send_rows(t + 1, jnp.concatenate([image[south_edge, :], image[north_edge, :]], 0))
         spaces.append(image)
     newest = len(spaces) - 1
     for i in range(len(spaces)):
@@ -542,14 +660,8 @@
 
     for_others(tell)
     for t in range(ITERS):
-
-        @pl.when(jnp.logical_not(east_border))
-        def _(t=t):
-            col_copy(t, 0).wait_send()
-
-        @pl.when(jnp.logical_not(west_border))
-        def _(t=t):
-            col_copy(t, 1).wait_send()
+        if t != 1:
+            for_sides(lambda side, t=t: col_copy(t, side).wait_send())
 
         @pl.when(has_north)
         def _(t=t):
@@ -559,14 +671,18 @@
         def _(t=t):
             row_copy(t, 1).wait_send()
 
+    for_rows(lambda side: mini_copy(side).wait_send())
+    for_sides(lambda side: edge_copy(side).wait_send())
+    for_corners(lambda k: corner_copy(k).wait_send(), True)
+
     @pl.when(border)
     def _():
-        wait_bytes(far_pack.at[:, own], far_send.at[0])
-        pl.when(gx == 0)(lambda: wait_bytes(far_pack.at[:, near_rest], far_send.at[0]))
+        pl.when(gx == 0)(lambda: wait_bytes(far_pack.at[:, alike], far_send.at[0]))
+        pl.when(gx > 0)(lambda: wait_bytes(far_pack.at[:, own], far_send.at[0]))
         pl.when(relays)(lambda: wait_bytes(far_pack.at[:, near_rest], relay_send))
+        pl.when(last)(lambda: wait_bytes(far_pack.at[:, alike], relay_send))
         wait_bytes(far_last, far_send.at[1])
         wait_bytes(near_pack.at[:, near_rest], near_send)
-        for_rows(lambda side: mini_copy(side).wait_send())
         c0, c1, c2 = edge_cols
         fields[1, c0, :] += strip[1, own, :]
         fields[2, c0, :] += strip[6, own, :]
@@ -641,11 +757,16 @@
             pltpu.VMEM((1, levels), f32),
             pltpu.VMEM((2 * levels, levels), f32),
             pltpu.VMEM((2, 2 * levels, 2 * levels), jnp.bfloat16),
-            pltpu.VMEM((ITERS, 4 * rows + 2 * cols, levels), f32),
+            pltpu.VMEM((ITERS, 6 * rows + 2 * cols, levels), f32),
             pltpu.VMEM((6, rows, levels), f32),
-            pltpu.VMEM((2, 8, levels), f32),
-            pltpu.VMEM((2, 8, levels), f32),
-            pltpu.VMEM((4, rows + 16, levels), f32),
+            pltpu.VMEM((2, 16, levels), f32),
+            pltpu.VMEM((2, 16, levels), f32),
+            pltpu.VMEM((2, 4, rows + 16, levels), f32),
+            pltpu.VMEM((2, 3, rows, levels), f32),
+            pltpu.VMEM((2, 3, rows, levels), f32),
+            pltpu.VMEM((4, 8, levels), f32),
+            pltpu.VMEM((4, 8, levels), f32),
+            pltpu.VMEM((2, rows + 16, levels), f32),
             pltpu.VMEM((ITERS, rows, levels), f32),
             pltpu.VMEM((ITERS, rows, levels), f32),
             pltpu.VMEM((ITERS, cols, levels), f32),
@@ -655,6 +776,7 @@
             pltpu.VMEM(column, f32),
             pltpu.VMEM((4,) + column, f32),
             pltpu.VMEM((10,) + column, f32),
+            pltpu.VMEM((2 * rows, levels), f32),
             pltpu.VMEM((2 * rows, levels), f32),
             pltpu.VMEM((16, levels), f32),
             pltpu.VMEM((n_gx * n_gy, 1, levels), f32),
@@ -671,6 +793,10 @@
             sems(()),
             sems((2,)),
             sems((2,)),
+            sems((2,)),
+            sems((2,)),
+            sems((4,)),
+            sems((4,)),
             sems((ITERS, 2)),
             sems((ITERS,)),
             sems((ITERS,)),

time: 21.4 us -> 20.6 us (0.963)
  Pallas kernels: 20.6 us -> 19.8 us
    pallas_call x1, Pallas kernels: 19.7 us -> 18.9 us  [on_device(): pl.pallas_call(functools.partial(kernel, n_gx, n_gy, rows), out_shape=(ba...]
where the time goes in v6:
time: 20.6 us; the launch traced here: 20.4 us
  Pallas kernels  19.8 us (96%)
  between operations  0.64 us (3%)
    pallas_call x1, Pallas kernels, on_device(): pl.pallas_call(functools.partial(kernel, n_gx, n_gy, rows), out_shape=(ba...  18.9 us
    pallas_call x1, Pallas kernels, on_device(): pl.pallas_call(functools.partial(finish, total_cells), out_shape=(jax.Sha...  0.86 us

profile of v6, /device:TPU:0, one launch (start us, length us, event | category | flops | bytes accessed | tf_op | source)
XLA Modules:
  0.0 20.4 jit_solution(14162976271940667115)
XLA Ops:
  0.6 18.9 %shard_map.85 = (f32[3,256,128]{2,1,0:T(8,128)S(1)}, f32[3,256,128]{2,1,0:T(8,128)S(1)}, f32[1,128]{1,0:T(1,128)S(1)}, f32[256,128]{1,0:T(8,128)S(1)}) custom-call(s32[2,64]{1,0:T(2,128)} %edge_table.1, f32[256,128]{1,0:T(8,128)} %bitcast.7, f32[256,128]{1,0:T(8,128)} %bitcast.8, f32[256,128]{1,0:T(8,128)} %bitcast.9, f32[1,128]{1,0:T(1,128)} %bitcast.10, ...), custom_call_target="tpu_custom_call" | custom-call | tf_op jit(solution)/shard_map/pallas_call | solution.py:749
  19.5 0.9 %shard_map.86 = (f32[256,128]{1,0:T(8,128)}, f32[256,128]{1,0:T(8,128)}, f32[1,3]{1,0:T(1,128)}) custom-call(f32[1,128]{1,0:T(1,128)S(1)} %get-tuple-element.10.all_totals, f32[256,128]{1,0:T(8,128)S(1)} %get-tuple-element.11.r0, f32[3,256,128]{2,1,0:T(8,128)S(1)} %get-tuple-element.12.fields, f32[3,256,128]{2,1,0:T(8,128)S(1)} %get-tuple-element.13.images), custom_call_target="tpu_custom_call" | custom-call | tf_op jit(solution)/shard_map/pallas_call | solution.py:819

commit v7 on v6

--- a/solution.py
+++ b/solution.py
@@ -35,6 +35,8 @@
     weights,
     frame_z,
     pack,
+    near_out,
+    near_coef,
     mini_out,
     mini_in,
     wide,
@@ -57,26 +59,18 @@
     partial,
     sums,
     edge_rows,
+    meter,
     load_sem,
-    col_send,
-    east_recv,
-    west_recv,
-    far_send,
+    small_sem,
+    sent,
+    sum_sent,
+    col_recv,
+    row_recv,
     far_recv,
-    relay_send,
     relay_recv,
-    near_send,
     near_recv,
-    mini_send,
     mini_recv,
-    edge_send,
-    edge_recv,
-    corner_send,
-    corner_recv,
-    row_send,
-    north_recv,
-    south_recv,
-    sum_send,
+    strip_recv,
     sum_recv,
 ):
     rows, levels = out_rows, r0.shape[-1]
@@ -111,13 +105,13 @@
 
     panel = lax.convert_element_type(gx >= half, jnp.int32)
     loads = [
-        pltpu.make_async_copy(right_side, r0, load_sem.at[0]),
-        pltpu.make_async_copy(precond.at[panel], matrix.at[pl.ds(0, levels)], load_sem.at[1]),
-        pltpu.make_async_copy(horizontal, horiz, load_sem.at[2]),
-        pltpu.make_async_copy(diagonal, diag, load_sem.at[3]),
-        pltpu.make_async_copy(vertical, vert, load_sem.at[4]),
-        pltpu.make_async_copy(edge_table, edge_rows, load_sem.at[5]),
-        pltpu.make_async_copy(precond.at[1 - panel], matrix.at[pl.ds(levels, levels)], load_sem.at[6]),
+        pltpu.make_async_copy(right_side, r0, load_sem),
+        pltpu.make_async_copy(precond.at[panel], matrix.at[pl.ds(0, levels)], load_sem),
+        pltpu.make_async_copy(horizontal, horiz, load_sem),
+        pltpu.make_async_copy(diagonal, diag, load_sem),
+        pltpu.make_async_copy(precond.at[1 - panel], matrix.at[pl.ds(levels, levels)], load_sem),
+        pltpu.make_async_copy(vertical, vert, small_sem.at[0]),
+        pltpu.make_async_copy(edge_table, edge_rows, small_sem.at[1]),
     ]
     for load in loads:
         load.start()
@@ -135,6 +129,18 @@
     first_row = pl.multiple_of(gy * rows, rows)
     own = pl.ds(first_row, rows)
     has_north, has_south = gy < n_gy - 1, gy > 0
+    between = has_north & has_south
+
+    def wait_count(count, sem):
+        part = meter.at[pl.ds(0, count)]
+        pltpu.make_async_copy(part, part, sem).wait()
+
+    def wait_cases(count, sem):
+        for n_sides, on_border in ((1, border), (2, jnp.logical_not(border))):
+            for n_rows, here in ((1, jnp.logical_not(between)), (2, between)):
+                pl.when(on_border & here)(
+                    functools.partial(wait_count, count(n_sides, n_rows), sem)
+                )
 
     @pl.when(jnp.logical_not(has_north))
     def _():
@@ -168,23 +174,21 @@
         return out[:, :levels] + out[:, levels:]
 
     def col_copy(t, side):
-        buffer, recv, x = (
-            (from_west, west_recv, east_x) if side == 0 else (from_east, east_recv, west_x)
-        )
+        buffer, x = (from_west, east_x) if side == 0 else (from_east, west_x)
         return pltpu.make_async_remote_copy(
             src_ref=frame_z.at[t, pl.ds(side * rows, rows)],
             dst_ref=buffer.at[t],
-            send_sem=col_send.at[t, side],
-            recv_sem=recv.at[t],
+            send_sem=sent,
+            recv_sem=col_recv.at[t // 2],
             device_id=(x, gy),
             device_id_type=MESH,
         )
 
     def far_copy(t, g):
         return pltpu.make_async_remote_copy(
-            src_ref=pack.at[pl.ds(0, 4)] if t == 0 else pack.at[5],
+            src_ref=pack.at[pl.ds(0, 4)] if t == 0 else pack.at[4],
             dst_ref=far_pack.at[:, own] if t == 0 else far_last.at[own],
-            send_sem=far_send.at[t],
+            send_sem=sent,
             recv_sem=far_recv.at[t],
             device_id=(far_x, g),
             device_id_type=MESH,
@@ -194,7 +198,7 @@
         return pltpu.make_async_remote_copy(
             src_ref=far_pack.at[:, block],
             dst_ref=far_pack.at[:, block],
-            send_sem=relay_send,
+            send_sem=sent,
             recv_sem=relay_recv,
             device_id=(gx, g),
             device_id_type=MESH,
@@ -202,9 +206,9 @@
 
     def near_copy(g):
         return pltpu.make_async_remote_copy(
-            src_ref=pack.at[pl.ds(0, 5)],
+            src_ref=near_out,
             dst_ref=near_pack.at[:, own],
-            send_sem=near_send,
+            send_sem=sent,
             recv_sem=near_recv,
             device_id=(gx, g),
             device_id_type=MESH,
@@ -214,23 +218,23 @@
         return pltpu.make_async_remote_copy(
             src_ref=mini_out.at[side],
             dst_ref=mini_in.at[side],
-            send_sem=mini_send.at[side],
-            recv_sem=mini_recv.at[side],
+            send_sem=sent,
+            recv_sem=mini_recv,
             device_id=(gx, gy + 1 if side == 0 else gy - 1),
             device_id_type=MESH,
         )
 
     def row_copy(t, side):
-        buffer, recv, y, row = (
-            (from_south, south_recv, gy + 1, 2 * rows + cols)
+        buffer, y, row = (
+            (from_south, gy + 1, 2 * rows + cols)
             if side == 0
-            else (from_north, north_recv, gy - 1, 2 * rows)
+            else (from_north, gy - 1, 2 * rows)
         )
         return pltpu.make_async_remote_copy(
             src_ref=frame_z.at[t, pl.ds(row, cols)],
             dst_ref=buffer.at[t],
-            send_sem=row_send.at[t, side],
-            recv_sem=recv.at[t],
+            send_sem=sent,
+            recv_sem=row_recv.at[t],
             device_id=(gx, y),
             device_id_type=MESH,
         )
@@ -239,8 +243,8 @@
         return pltpu.make_async_remote_copy(
             src_ref=edge_out.at[side],
             dst_ref=edge_in.at[1 - side],
-            send_sem=edge_send.at[side],
-            recv_sem=edge_recv.at[1 - side],
+            send_sem=sent,
+            recv_sem=strip_recv,
             device_id=(east_x if side == 0 else west_x, gy),
             device_id_type=MESH,
         )
@@ -249,8 +253,8 @@
         return pltpu.make_async_remote_copy(
             src_ref=corner_out.at[k],
             dst_ref=corner_in.at[k],
-            send_sem=corner_send.at[k],
-            recv_sem=corner_recv.at[k],
+            send_sem=sent,
+            recv_sem=strip_recv,
             device_id=(west_x if k < 2 else east_x, gy + 1 if k % 2 == 0 else gy - 1),
             device_id_type=MESH,
         )
@@ -298,23 +302,26 @@
                 picks = [(0, first), (0, second), (1, first), (2, first), (3, first)]
                 for k, (item, row) in enumerate(picks):
                     mini_out[to, pl.ds(8 * side + k, 1), :] = items[item][row : row + 1]
-                mini_out[to, pl.ds(8 * side + 5, 3), :] = jnp.zeros((3, levels), jnp.float32)
+                next_horiz = horiz[pl.ds(first * cols + (1 if side else cols - 2), 1), :]
+                mini_out[to, pl.ds(8 * side + 5, 1), :] = next_horiz
+                mini_out[to, pl.ds(8 * side + 6, 2), :] = jnp.zeros((2, levels), jnp.float32)
                 corner_out[2 * (1 - side) + to] = jnp.zeros((8, levels), jnp.float32)
                 corner_out[2 * (1 - side) + to, pl.ds(0, 1), :] = items[0][first : first + 1]
         beyond[...] = jnp.zeros_like(beyond)
 
     def fill_packs():
         c0, c1, c2 = edge_cols
-        items = [
-            frame_z[0, pl.ds(side * rows, rows), :],
-            frame_z[0, pl.ds(inward + side * rows, rows), :],
-            horiz[c0, :],
-            diag[c0, :],
-            horiz[c1, :],
-        ]
-        for k, item in enumerate(items):
+        z_edge = frame_z[0, pl.ds(side * rows, rows), :]
+        h_edge, d_edge = horiz[c0, :], diag[c0, :]
+        z_next = frame_z[0, pl.ds(inward + side * rows, rows), :]
+        for k, item in enumerate([z_edge, z_next, h_edge, d_edge]):
             pack[k] = item
+        for k, item in enumerate([z_edge, h_edge]):
+            near_out[k] = item
             near_pack[k, own, :] = item
+        for k, item in enumerate([d_edge, horiz[c1, :]]):
+            near_coef[k] = jnp.zeros_like(near_coef[k])
+            near_coef[k, own, :] = item
 
     def send_first(frame):
         frame_z[0] = precondition(frame)
@@ -324,8 +331,8 @@
 
         @pl.when(gx == 0)
         def _():
-            for j in range(0, n_gy, 2):
-                far_copy(0, lax.rem(gy + j, n_gy)).start()
+            for g in range(1, n_gy, 2):
+                far_copy(0, g).start()
 
         for_sides(lambda side: col_copy(0, side).start())
         for_rows(lambda side: mini_copy(side).start())
@@ -333,11 +340,7 @@
         for_corners(lambda k: corner_copy(k).start(), True)
         for_sides(lambda side: edge_copy(side).start())
 
-        @pl.when(border)
-        def _():
-            pl.when(gx > 0)(lambda: far_copy(0, gy).start())
-            for j in range(1, n_gy):
-                near_copy(lax.rem(gy + j, n_gy)).start()
+        pl.when(border & (gx > 0))(lambda: far_copy(0, gy).start())
 
     def send_rows(t, frame):
         frame_z[t, pl.ds(2 * rows, 2 * cols), :] = precondition(frame)
@@ -346,20 +349,17 @@
     def send_far_last():
         for j in sorted(range(n_gy), key=lambda j: abs(2 * j - n_gy)):
             far_copy(1, lax.rem(gy + j, n_gy)).start()
+        for j in range(1, n_gy):
+            near_copy(lax.rem(gy + j, n_gy)).start()
 
     def receive_rows(t):
-        @pl.when(has_north)
-        def _():
-            row_copy(t, 1).wait_recv()
-
-        @pl.when(has_south)
-        def _():
-            row_copy(t, 0).wait_recv()
+        wait_cases(lambda sides, beside: beside * cols, row_recv.at[t])
 
     def receive_cols(t):
+        wait_cases(lambda sides, beside: sides * rows, col_recv.at[t // 2])
+
         def take(side):
             buffer = from_west if side else from_east
-            col_copy(t, 1 - side).wait_recv()
             outside[pl.ds(side * rows, rows), :] = buffer[t]
             if t == 0:
                 beyond[side, mid, :] = buffer[t]
@@ -429,12 +429,12 @@
     relays = border & jnp.logical_not(last)
     alike = pl.ds(0, n_gy // 2 * rows)
 
+    crosses = last & (lax.rem(gy, 2) == 1)
+    crossed = last & (lax.rem(gy, 2) == 0)
+
     def relay_across():
-        wait_bytes(far_pack.at[:, alike], far_recv.at[0])
-        for k in range(n_gy // 2):
-            g = lax.rem(gy, 2) + 2 * k
-            block = pl.ds(pl.multiple_of(g * rows, rows), rows)
-            relay_copy(gy + 1 - 2 * lax.rem(gy, 2), block).start()
+        wait_bytes(far_pack, far_recv.at[0])
+        relay_copy(gy - 1, pl.ds(0, tall)).start()
 
     def relay():
         wait_bytes(far_pack.at[:, own], far_recv.at[0])
@@ -452,17 +452,19 @@
     def look_ahead():
         c1 = edge_cols[1]
 
-        def take(direction, near, far):
-            mini_copy(direction).wait_recv()
-            for side in range(2):
-                row = mini_in.at[direction]
-                wide[side, 0, pl.ds(near, 1), :] = row[pl.ds(8 * side, 1), :]
-                wide[side, 0, pl.ds(far, 1), :] = row[pl.ds(8 * side + 1, 1), :]
+        def take(direction, near, far, row):
+            for k in range(2):
+                near_coef[k, pl.ds(row, 1), :] = mini_in[direction, pl.ds(8 * side + 4 + k, 1), :]
+            for k_side in range(2):
+                given = mini_in.at[direction]
+                wide[k_side, 0, pl.ds(near, 1), :] = given[pl.ds(8 * k_side, 1), :]
+                wide[k_side, 0, pl.ds(far, 1), :] = given[pl.ds(8 * k_side + 1, 1), :]
                 for k in (1, 2, 3):
-                    wide[side, k, pl.ds(near, 1), :] = row[pl.ds(8 * side + k + 1, 1), :]
-
-        pl.when(has_south)(functools.partial(take, 0, 7, 6))
-        pl.when(has_north)(functools.partial(take, 1, 8 + rows, 9 + rows))
+                    wide[k_side, k, pl.ds(near, 1), :] = given[pl.ds(8 * k_side + k + 1, 1), :]
+
+        wait_cases(lambda sides, beside: 16 * beside, mini_recv)
+        pl.when(has_south)(functools.partial(take, 0, 7, 6, first_row - 1))
+        pl.when(has_north)(functools.partial(take, 1, 8 + rows, 9 + rows, first_row + rows))
         z_edge, z_next, h_edge, d_edge = (wide[side, k] for k in range(4))
         v_edge = (
             d_edge * z_edge
@@ -479,16 +481,17 @@
         z_edge, z_next = z[: rows + 16], z[rows + 16 :]
         beside = next_to(z_edge)[8 : 8 + rows] + z_next
         z_edge = z_edge[8 : 8 + rows]
+        near_out[2] = z_edge
+        near_pack[2, own, :] = z_edge
         h_own, d_own = h_edge[8 : 8 + rows], d_edge[8 : 8 + rows]
         v = d_own * z_edge + h_own * (4.0 * z_edge - beside) + column_part(z_edge)
-        pack[5] = precondition(v)
+        pack[4] = precondition(v)
         pl.when(border)(send_far_last)
 
     def look_across():
-        for_sides(lambda side: edge_copy(1 - side).wait_recv())
+        wait_cases(lambda sides, beside: sides * (3 * rows + 8 * beside), strip_recv)
 
         def take(k):
-            corner_copy(k).wait_recv()
             row = 8 + rows if k % 2 else 7
             beyond[k // 2, pl.ds(row, 1), :] = corner_in[k, pl.ds(0, 1), :]
 
@@ -533,27 +536,26 @@
     def correct_early():
         @pl.when(border)
         def _():
-            pl.when(last)(lambda: wait_bytes(far_pack.at[:, alike], relay_recv))
+            pl.when(crossed)(lambda: wait_bytes(far_pack, relay_recv))
             pl.when(relays)(lambda: wait_bytes(far_pack.at[:, near_rest], relay_recv))
             wait_bytes(near_pack.at[:, near_rest], near_recv)
 
         gather_rows(0, tall, [(0, far_pack.at[0]), (1, near_pack.at[0])])
-        h_near, d_near = near_pack[2], near_pack[3]
+        h_near, d_near = near_pack[1], near_coef[0]
         h_far, d_far = far_pack[2], far_pack[3]
         b_near, b_far = -(h_near * gathered[0]), -(h_far * gathered[1])
-        v_near = stencil(near_pack[0], d_near, h_near) - h_near * near_pack[1] + b_near
         v_far = stencil(far_pack[0], d_far, h_far) - h_far * far_pack[1] + b_far
-        near = precondition(jnp.concatenate([b_near, v_near], 0))
+        w_near = precondition(b_near)
         far = precondition(jnp.concatenate([b_far, v_far], 0), 1)
-        w_near, w_far = near[:tall], far[:tall]
+        w_far = far[:tall]
         strip[0] = b_near
         strip[1] = w_near
         strip[3] = far[tall:]
-        strip[4] = near[tall:]
+        strip[4] = near_pack[2] + w_near
         gather_rows(0, tall, [(0, strip.at[3]), (1, strip.at[4])])
         b_near = stencil(w_near, d_near, h_near) - h_near * gathered[0]
         b_far = stencil(w_far, d_far, h_far) - h_far * gathered[1]
-        b_next = -(near_pack[4] * w_near)
+        b_next = -(near_coef[1] * w_near)
         near = precondition(jnp.concatenate([b_near, b_next], 0))
         w_edge, w_next = near[:tall], near[tall:]
         strip[3] = b_near
@@ -594,7 +596,8 @@
             if j > 0:
                 partial[pl.ds(k, 1), :] += product(after[i], after[j]) - product(before[i], before[j])
 
-    for load in loads:
+    wait_count(3 * cells + 2 * levels, load_sem)
+    for load in loads[5:]:
         load.wait()
     prepare_weights()
     terms = {}
@@ -617,7 +620,7 @@
             pl.when(relays)(relay)
             look_across()
         if t == 2:
-            pl.when(last)(relay_across)
+            pl.when(crosses)(relay_across)
             correct_early()
         receive_rows(t)
         image[south_edge, :] = image[south_edge, :] - horiz[south_edge, :] * from_south[t]
@@ -652,37 +655,33 @@
         pltpu.make_async_remote_copy(
             src_ref=sums.at[me],
             dst_ref=sums.at[me],
-            send_sem=sum_send,
+            send_sem=sum_sent,
             recv_sem=sum_recv,
             device_id=(x, y),
             device_id_type=MESH,
         ).start()
 
     for_others(tell)
-    for t in range(ITERS):
-        if t != 1:
-            for_sides(lambda side, t=t: col_copy(t, side).wait_send())
-
-        @pl.when(has_north)
-        def _(t=t):
-            row_copy(t, 0).wait_send()
-
-        @pl.when(has_south)
-        def _(t=t):
-            row_copy(t, 1).wait_send()
-
-    for_rows(lambda side: mini_copy(side).wait_send())
-    for_sides(lambda side: edge_copy(side).wait_send())
-    for_corners(lambda k: corner_copy(k).wait_send(), True)
+    def all_sent(sides, beside, border_part):
+        per_side = 5 * rows + 8 * beside
+        return sides * per_side + beside * (ITERS * cols + 16) + border_part * rows
+
+    common = n_gy + 3 * (n_gy - 1)
+    first, inner = gx == 0, border & jnp.logical_not(last | (gx == 0))
+    for condition, sides, border_part in (
+        (jnp.logical_not(border), 2, 0),
+        (first, 1, common + 2 * n_gy + 4 * (n_gy - 1)),
+        (inner, 1, common + 4 + 4 * (n_gy - 1)),
+        (crosses, 1, common + 4 + 4 * n_gy),
+        (crossed, 1, common + 4),
+    ):
+        for beside, here in ((1, jnp.logical_not(between)), (2, between)):
+            pl.when(condition & here)(
+                functools.partial(wait_count, all_sent(sides, beside, border_part), sent)
+            )
 
     @pl.when(border)
     def _():
-        pl.when(gx == 0)(lambda: wait_bytes(far_pack.at[:, alike], far_send.at[0]))
-        pl.when(gx > 0)(lambda: wait_bytes(far_pack.at[:, own], far_send.at[0]))
-        pl.when(relays)(lambda: wait_bytes(far_pack.at[:, near_rest], relay_send))
-        pl.when(last)(lambda: wait_bytes(far_pack.at[:, alike], relay_send))
-        wait_bytes(far_last, far_send.at[1])
-        wait_bytes(near_pack.at[:, near_rest], near_send)
         c0, c1, c2 = edge_cols
         fields[1, c0, :] += strip[1, own, :]
         fields[2, c0, :] += strip[6, own, :]
@@ -691,7 +690,7 @@
     others = sums.at[pl.ds(0, n_all - 1)]
     wait_bytes(others, sum_recv)
     out_totals[...] = jnp.sum(sums[...], axis=0)
-    wait_bytes(others, sum_send)
+    wait_bytes(others, sum_sent)
 
 
 def finish(
@@ -745,6 +744,7 @@
     block = (rows * cols, levels)
     column = (n_gy * rows, levels)
     sems = pltpu.SemaphoreType.DMA
+    meter_rows = 3 * rows * cols + 2 * levels + (16 + 10 * n_gy) * rows + 8 * cols + 64
     basis = pltpu.VMEM((ITERS,) + block, f32)
     fields, images, totals, start = pl.pallas_call(
         functools.partial(kernel, n_gx, n_gy, rows),
@@ -758,7 +758,9 @@
             pltpu.VMEM((2 * levels, levels), f32),
             pltpu.VMEM((2, 2 * levels, 2 * levels), jnp.bfloat16),
             pltpu.VMEM((ITERS, 6 * rows + 2 * cols, levels), f32),
-            pltpu.VMEM((6, rows, levels), f32),
+            pltpu.VMEM((5, rows, levels), f32),
+            pltpu.VMEM((3, rows, levels), f32),
+            pltpu.VMEM((2,) + column, f32),
             pltpu.VMEM((2, 16, levels), f32),
             pltpu.VMEM((2, 16, levels), f32),
             pltpu.VMEM((2, 4, rows + 16, levels), f32),
@@ -772,7 +774,7 @@
             pltpu.VMEM((ITERS, cols, levels), f32),
             pltpu.VMEM((ITERS, cols, levels), f32),
             pltpu.VMEM((4,) + column, f32),
-            pltpu.VMEM((5,) + column, f32),
+            pltpu.VMEM((3,) + column, f32),
             pltpu.VMEM(column, f32),
             pltpu.VMEM((4,) + column, f32),
             pltpu.VMEM((10,) + column, f32),
@@ -781,25 +783,17 @@
             pltpu.VMEM((16, levels), f32),
             pltpu.VMEM((n_gx * n_gy, 1, levels), f32),
             pltpu.SMEM(edge_rows.shape, jnp.int32),
-            sems((7,)),
-            sems((ITERS, 2)),
+            pltpu.VMEM((meter_rows, levels), f32),
+            sems(()),
+            sems((2,)),
+            sems(()),
+            sems(()),
+            sems((2,)),
             sems((ITERS,)),
-            sems((ITERS,)),
-            sems((2,)),
             sems((2,)),
             sems(()),
             sems(()),
             sems(()),
-            sems(()),
-            sems((2,)),
-            sems((2,)),
-            sems((2,)),
-            sems((2,)),
-            sems((4,)),
-            sems((4,)),
-            sems((ITERS, 2)),
-            sems((ITERS,)),
-            sems((ITERS,)),
             sems(()),
             sems(()),
         ],

time: 20.6 us -> 20.1 us (0.976)
  Pallas kernels: 19.8 us -> 19.4 us
    pallas_call x1, Pallas kernels: 18.9 us -> 18.5 us  [on_device(): pl.pallas_call(functools.partial(kernel, n_gx, n_gy, rows), out_shape=(ba...]
where the time goes in v7:
time: 20.1 us; the launch traced here: 20 us
  Pallas kernels  19.4 us (97%)
  between operations  0.64 us (3%)
    pallas_call x1, Pallas kernels, on_device(): pl.pallas_call(functools.partial(kernel, n_gx, n_gy, rows), out_shape=(ba...  18.5 us
    pallas_call x1, Pallas kernels, on_device(): pl.pallas_call(functools.partial(finish, total_cells), out_shape=(jax.Sha...  0.86 us

profile of v7, /device:TPU:0, one launch (start us, length us, event | category | flops | bytes accessed | tf_op | source)
XLA Modules:
  0.0 20.0 jit_solution(3589882584224900879)
XLA Ops:
  0.6 18.5 %shard_map.85 = (f32[3,256,128]{2,1,0:T(8,128)S(1)}, f32[3,256,128]{2,1,0:T(8,128)S(1)}, f32[1,128]{1,0:T(1,128)S(1)}, f32[256,128]{1,0:T(8,128)S(1)}) custom-call(s32[2,64]{1,0:T(2,128)} %edge_table.1, f32[256,128]{1,0:T(8,128)} %bitcast.7, f32[256,128]{1,0:T(8,128)} %bitcast.8, f32[256,128]{1,0:T(8,128)} %bitcast.9, f32[1,128]{1,0:T(1,128)} %bitcast.10, ...), custom_call_target="tpu_custom_call" | custom-call | tf_op jit(solution)/shard_map/pallas_call | solution.py:749
  19.1 0.9 %shard_map.86 = (f32[256,128]{1,0:T(8,128)}, f32[256,128]{1,0:T(8,128)}, f32[1,3]{1,0:T(1,128)}) custom-call(f32[1,128]{1,0:T(1,128)S(1)} %get-tuple-element.10.all_totals, f32[256,128]{1,0:T(8,128)S(1)} %get-tuple-element.11.r0, f32[3,256,128]{2,1,0:T(8,128)S(1)} %get-tuple-element.12.fields, f32[3,256,128]{2,1,0:T(8,128)S(1)} %get-tuple-element.13.images), custom_call_target="tpu_custom_call" | custom-call | tf_op jit(solution)/shard_map/pallas_call | solution.py:813

commit v8 on v7

--- a/solution.py
+++ b/solution.py
@@ -57,6 +57,7 @@
     strip_out,
     outside,
     partial,
+    extra,
     sums,
     edge_rows,
     meter,
@@ -151,6 +152,7 @@
         from_south[...] = jnp.zeros_like(from_south)
 
     outside[...] = jnp.zeros_like(outside)
+    extra[...] = jnp.zeros_like(extra)
 
     def split(v):
         high = v.astype(jnp.bfloat16)
@@ -329,13 +331,14 @@
         pl.when(border)(fill_packs)
         pl.semaphore_wait(barrier, n_all - 1)
 
+        for_rows(lambda side: mini_copy(side).start())
+
         @pl.when(gx == 0)
         def _():
             for g in range(1, n_gy, 2):
                 far_copy(0, g).start()
 
         for_sides(lambda side: col_copy(0, side).start())
-        for_rows(lambda side: mini_copy(side).start())
         for_rows(lambda side: row_copy(0, side).start())
         for_corners(lambda k: corner_copy(k).start(), True)
         for_sides(lambda side: edge_copy(side).start())
@@ -349,6 +352,8 @@
     def send_far_last():
         for j in sorted(range(n_gy), key=lambda j: abs(2 * j - n_gy)):
             far_copy(1, lax.rem(gy + j, n_gy)).start()
+
+    def send_near():
         for j in range(1, n_gy):
             near_copy(lax.rem(gy + j, n_gy)).start()
 
@@ -566,35 +571,55 @@
         strip[8] = along(w_next)
         strip[9] = stencil(w_edge, d_near, h_near) - h_near * w_next
 
-    def correct_third():
-        c0, c1, c2 = edge_cols
-        w_edge, w_next, beside = strip[6, own, :], strip[7, own, :], strip[8, own, :]
-        h1 = horiz[c1, :]
-        later = diag[c1, :] * w_next + h1 * (4.0 * w_next - beside - w_edge) + column_part(w_next)
-        b_third = -(horiz[c2, :] * w_next)
-        gather_rows(first_row, rows, [(2, strip.at[5])])
-        wait_bytes(far_last, far_recv.at[1])
-        gather_rows(first_row, rows, [(3, far_last)])
-        across = gathered[2, pl.ds(0, rows), :] + gathered[3, pl.ds(0, rows), :]
-        b_edge = strip[9, own, :] - horiz[c0, :] * across
+    def strip_of(ref):
+        return jnp.concatenate([ref[c, :] for c in edge_cols], 0)
+
+    def add_to(key, value):
+        extra[pl.ds(KEYS.index(key), 1), :] += value
+
+    def correct_two():
         none = jnp.zeros((rows, levels), jnp.float32)
         changes = [
             [strip[0, own, :], none, none],
             [strip[3, own, :], strip[4, own, :], none],
-            [b_edge, later, b_third],
         ]
-        before = [jnp.concatenate([r0[c, :] for c in edge_cols], 0)]
+        before = [strip_of(r0)]
         after = [before[0]]
-        for t in range(ITERS):
-            old = jnp.concatenate([images[t, c, :] for c in edge_cols], 0)
+        for t in range(2):
+            old = strip_of(images.at[t])
             new = old + jnp.concatenate(changes[t], 0)
             before.append(old)
             after.append(new)
             for k in range(t + 1):
                 images[t, edge_cols[k], :] = new[k * rows : (k + 1) * rows]
-        for k, (i, j) in enumerate(KEYS):
-            if j > 0:
-                partial[pl.ds(k, 1), :] += product(after[i], after[j]) - product(before[i], before[j])
+        for i, j in KEYS:
+            if 0 < j < 3:
+                add_to((i, j), product(after[i], after[j]) - product(before[i], before[j]))
+        gather_rows(first_row, rows, [(2, strip.at[5])])
+
+    def correct_third():
+        c0, c1, c2 = edge_cols
+        w_edge, w_next, beside = strip[6, own, :], strip[7, own, :], strip[8, own, :]
+        h0, h1 = horiz[c0, :], horiz[c1, :]
+        later = diag[c1, :] * w_next + h1 * (4.0 * w_next - beside - w_edge) + column_part(w_next)
+        rest = jnp.concatenate([later, -(horiz[c2, :] * w_next)], 0)
+        spaces_here = [strip_of(r0), strip_of(images.at[0]), strip_of(images.at[1])]
+        old = strip_of(images.at[2])
+        new_rest = old[rows:] + rest
+        images[2, c1, :] = new_rest[:rows]
+        images[2, c2, :] = new_rest[rows:]
+        for i, space in enumerate(spaces_here):
+            add_to((i, 3), product(space[rows:], rest))
+        add_to((3, 3), product(new_rest, new_rest) - product(old, old))
+        base = strip[9, own, :] - h0 * gathered[2, pl.ds(0, rows), :]
+        wait_bytes(far_last, far_recv.at[1])
+        gather_rows(first_row, rows, [(3, far_last)])
+        b_edge = base - h0 * gathered[3, pl.ds(0, rows), :]
+        new = old[:rows] + b_edge
+        images[2, c0, :] = new
+        for i, space in enumerate(spaces_here):
+            add_to((i, 3), product(space[:rows], b_edge))
+        add_to((3, 3), product(new, new))
 
     wait_count(3 * cells + 2 * levels, load_sem)
     for load in loads[5:]:
@@ -622,6 +647,7 @@
         if t == 2:
             pl.when(crosses)(relay_across)
             correct_early()
+            pl.when(border)(correct_two)
         receive_rows(t)
         image[south_edge, :] = image[south_edge, :] - horiz[south_edge, :] * from_south[t]
         image[north_edge, :] = image[north_edge, :] - horiz[north_edge, :] * from_north[t]
@@ -633,6 +659,8 @@
         image[west_edge, :] = edges[rows:]
         if t < ITERS - 1:
             send_rows(t + 1, jnp.concatenate([image[south_edge, :], image[north_edge, :]], 0))
+        if t == 0:
+            pl.when(border)(send_near)
         spaces.append(image)
     newest = len(spaces) - 1
     for i in range(len(spaces)):
@@ -647,7 +675,7 @@
     height = -(-len(KEYS) // 8) * 8
     row_id = lax.broadcasted_iota(jnp.int32, (height, levels), 0)
     lane = lax.broadcasted_iota(jnp.int32, (height, levels), 1)
-    stacked = jnp.where(row_id < len(KEYS), partial[...], 0.0)
+    stacked = jnp.where(row_id < len(KEYS), partial[...] + extra[...], 0.0)
     summed = jnp.sum(stacked, axis=1, keepdims=True)
     sums[me] = jnp.sum(jnp.where(lane == row_id, summed, 0.0), axis=0, keepdims=True)
 
@@ -780,6 +808,7 @@
             pltpu.VMEM((10,) + column, f32),
             pltpu.VMEM((2 * rows, levels), f32),
             pltpu.VMEM((2 * rows, levels), f32),
+            pltpu.VMEM((16, levels), f32),
             pltpu.VMEM((16, levels), f32),
             pltpu.VMEM((n_gx * n_gy, 1, levels), f32),
             pltpu.SMEM(edge_rows.shape, jnp.int32),

time: 20.1 us -> 20.1 us (level)
  no operation moved by 1% of the time
where the time goes in v8:
time: 20.1 us; the launch traced here: 19.9 us
  Pallas kernels  19.3 us (96%)
  between operations  0.64 us (3%)
    pallas_call x1, Pallas kernels, on_device(): pl.pallas_call(functools.partial(kernel, n_gx, n_gy, rows), out_shape=(ba...  18.4 us
    pallas_call x1, Pallas kernels, on_device(): pl.pallas_call(functools.partial(finish, total_cells), out_shape=(jax.Sha...  0.86 us

profile of v8, /device:TPU:0, one launch (start us, length us, event | category | flops | bytes accessed | tf_op | source)
XLA Modules:
  0.0 19.9 jit_solution(14330327767951974737)
XLA Ops:
  0.6 18.4 %shard_map.85 = (f32[3,256,128]{2,1,0:T(8,128)S(1)}, f32[3,256,128]{2,1,0:T(8,128)S(1)}, f32[1,128]{1,0:T(1,128)S(1)}, f32[256,128]{1,0:T(8,128)S(1)}) custom-call(s32[2,64]{1,0:T(2,128)} %edge_table.1, f32[256,128]{1,0:T(8,128)} %bitcast.7, f32[256,128]{1,0:T(8,128)} %bitcast.8, f32[256,128]{1,0:T(8,128)} %bitcast.9, f32[1,128]{1,0:T(1,128)} %bitcast.10, ...), custom_call_target="tpu_custom_call" | custom-call | tf_op jit(solution)/shard_map/pallas_call | solution.py:777
  19.1 0.9 %shard_map.86 = (f32[256,128]{1,0:T(8,128)}, f32[256,128]{1,0:T(8,128)}, f32[1,3]{1,0:T(1,128)}) custom-call(f32[1,128]{1,0:T(1,128)S(1)} %get-tuple-element.10.all_totals, f32[256,128]{1,0:T(8,128)S(1)} %get-tuple-element.11.r0, f32[3,256,128]{2,1,0:T(8,128)S(1)} %get-tuple-element.12.fields, f32[3,256,128]{2,1,0:T(8,128)S(1)} %get-tuple-element.13.images), custom_call_target="tpu_custom_call" | custom-call | tf_op jit(solution)/shard_map/pallas_call | solution.py:842

commit v9 on v8

--- a/solution.py
+++ b/solution.py
@@ -158,19 +158,19 @@
         high = v.astype(jnp.bfloat16)
         return high, (v - high.astype(jnp.float32)).astype(jnp.bfloat16)
 
-    def prepare_weights():
-        for which in range(2):
-            for part, value in enumerate(split(matrix[pl.ds(which * levels, levels), :])):
-                for twice in range(2):
-                    weights[
-                        which, pl.ds(part * levels, levels), pl.ds(twice * levels, levels)
-                    ] = value
+    def prepare_weights(which):
+        turned = jnp.transpose(matrix[pl.ds(which * levels, levels), :])
+        for part, value in enumerate(split(turned)):
+            for twice in range(2):
+                weights[
+                    which, pl.ds(twice * levels, levels), pl.ds(part * levels, levels)
+                ] = value
 
     def precondition(v, which=0):
         out = lax.dot_general(
             jnp.concatenate(split(v), 1),
             weights[which],
-            (((1,), (1,)), ((), ())),
+            (((1,), (0,)), ((), ())),
             preferred_element_type=jnp.float32,
         )
         return out[:, :levels] + out[:, levels:]
@@ -333,25 +333,25 @@
 
         for_rows(lambda side: mini_copy(side).start())
 
-        @pl.when(gx == 0)
-        def _():
-            for g in range(1, n_gy, 2):
-                far_copy(0, g).start()
-
+        pl.when(gx == 0)(send_far_pack)
         for_sides(lambda side: col_copy(0, side).start())
         for_rows(lambda side: row_copy(0, side).start())
         for_corners(lambda k: corner_copy(k).start(), True)
         for_sides(lambda side: edge_copy(side).start())
 
-        pl.when(border & (gx > 0))(lambda: far_copy(0, gy).start())
+        pl.when(border & (gx > 0))(send_far_pack)
 
     def send_rows(t, frame):
         frame_z[t, pl.ds(2 * rows, 2 * cols), :] = precondition(frame)
         for_rows(lambda side: row_copy(t, side).start())
 
+    def send_far_pack():
+        for g in range(1, n_gy, 2):
+            far_copy(0, g).start()
+
     def send_far_last():
-        for j in sorted(range(n_gy), key=lambda j: abs(2 * j - n_gy)):
-            far_copy(1, lax.rem(gy + j, n_gy)).start()
+        for g in sorted(range(n_gy), key=lambda g: g % 2):
+            far_copy(1, g).start()
 
     def send_near():
         for j in range(1, n_gy):
@@ -431,21 +431,12 @@
 
     near_rest = pl.ds(0, (n_gy - 1) * rows)
     last = gx == n_gx - 1
-    relays = border & jnp.logical_not(last)
-    alike = pl.ds(0, n_gy // 2 * rows)
-
-    crosses = last & (lax.rem(gy, 2) == 1)
-    crossed = last & (lax.rem(gy, 2) == 0)
+    crosses = border & (lax.rem(gy, 2) == 1)
+    crossed = border & (lax.rem(gy, 2) == 0)
 
     def relay_across():
         wait_bytes(far_pack, far_recv.at[0])
         relay_copy(gy - 1, pl.ds(0, tall)).start()
-
-    def relay():
-        wait_bytes(far_pack.at[:, own], far_recv.at[0])
-        for j in sorted(range(1, n_gy), key=lambda j: abs(2 * j - n_gy)):
-            relay_copy(lax.rem(gy + j, n_gy), own).start()
-
 
     def next_to(w):
         return pltpu.roll(w, w.shape[0] - 1, 0) + pltpu.roll(w, 1, 0)
@@ -539,13 +530,13 @@
         for_sides(give)
 
     def correct_early():
+        pl.when(border)(lambda: wait_bytes(near_pack.at[:, near_rest], near_recv))
+        gather_rows(0, tall, [(1, near_pack.at[0])])
+
         @pl.when(border)
         def _():
             pl.when(crossed)(lambda: wait_bytes(far_pack, relay_recv))
-            pl.when(relays)(lambda: wait_bytes(far_pack.at[:, near_rest], relay_recv))
-            wait_bytes(near_pack.at[:, near_rest], near_recv)
-
-        gather_rows(0, tall, [(0, far_pack.at[0]), (1, near_pack.at[0])])
+        gather_rows(0, tall, [(0, far_pack.at[0])])
         h_near, d_near = near_pack[1], near_coef[0]
         h_far, d_far = far_pack[2], far_pack[3]
         b_near, b_far = -(h_near * gathered[0]), -(h_far * gathered[1])
@@ -624,7 +615,7 @@
     wait_count(3 * cells + 2 * levels, load_sem)
     for load in loads[5:]:
         load.wait()
-    prepare_weights()
+    prepare_weights(0)
     terms = {}
     spaces = [r0]
     frame = [edge_columns(r0), r0[south_edge, :], r0[north_edge, :]]
@@ -640,9 +631,10 @@
             terms[(i, newest)] = product(spaces[i][...], spaces[newest][...])
         image[...] = inner_image(z)
         if t == 0:
+            prepare_weights(1)
             look_ahead()
+            pl.when(border & jnp.logical_not(last))(send_near)
         if t == 1:
-            pl.when(relays)(relay)
             look_across()
         if t == 2:
             pl.when(crosses)(relay_across)
@@ -660,7 +652,7 @@
         if t < ITERS - 1:
             send_rows(t + 1, jnp.concatenate([image[south_edge, :], image[north_edge, :]], 0))
         if t == 0:
-            pl.when(border)(send_near)
+            pl.when(last)(send_near)
         spaces.append(image)
     newest = len(spaces) - 1
     for i in range(len(spaces)):
@@ -689,19 +681,25 @@
             device_id_type=MESH,
         ).start()
 
-    for_others(tell)
+    def tell_all(x, carry):
+        for y in range(n_gy):
+            pl.when(me != x * n_gy + y)(functools.partial(tell, x, y))
+        return carry
+
+    if n_all <= 64:
+        for x in range(n_gx):
+            tell_all(x, 0)
+    else:
+        lax.fori_loop(0, n_gx, tell_all, 0)
     def all_sent(sides, beside, border_part):
         per_side = 5 * rows + 8 * beside
         return sides * per_side + beside * (ITERS * cols + 16) + border_part * rows
 
-    common = n_gy + 3 * (n_gy - 1)
-    first, inner = gx == 0, border & jnp.logical_not(last | (gx == 0))
+    common = n_gy + 3 * (n_gy - 1) + 2 * n_gy
     for condition, sides, border_part in (
         (jnp.logical_not(border), 2, 0),
-        (first, 1, common + 2 * n_gy + 4 * (n_gy - 1)),
-        (inner, 1, common + 4 + 4 * (n_gy - 1)),
-        (crosses, 1, common + 4 + 4 * n_gy),
-        (crossed, 1, common + 4),
+        (crosses, 1, common + 4 * n_gy),
+        (crossed, 1, common),
     ):
         for beside, here in ((1, jnp.logical_not(between)), (2, between)):
             pl.when(condition & here)(

time: 20.1 us -> 20 us (level)
  no operation moved by 1% of the time
where the time goes in v9:
time: 20 us; the launch traced here: 19.9 us
  Pallas kernels  19.2 us (96%)
  between operations  0.64 us (3%)
    pallas_call x1, Pallas kernels, on_device(): pl.pallas_call(functools.partial(kernel, n_gx, n_gy, rows), out_shape=(ba...  18.4 us
    pallas_call x1, Pallas kernels, on_device(): pl.pallas_call(functools.partial(finish, total_cells), out_shape=(jax.Sha...  0.86 us

profile of v9, /device:TPU:0, one launch (start us, length us, event | category | flops | bytes accessed | tf_op | source)
XLA Modules:
  0.0 19.9 jit_solution(15407996753611621584)
XLA Ops:
  0.6 18.4 %shard_map.85 = (f32[3,256,128]{2,1,0:T(8,128)S(1)}, f32[3,256,128]{2,1,0:T(8,128)S(1)}, f32[1,128]{1,0:T(1,128)S(1)}, f32[256,128]{1,0:T(8,128)S(1)}) custom-call(s32[2,64]{1,0:T(2,128)} %edge_table.1, f32[256,128]{1,0:T(8,128)} %bitcast.7, f32[256,128]{1,0:T(8,128)} %bitcast.8, f32[256,128]{1,0:T(8,128)} %bitcast.9, f32[1,128]{1,0:T(1,128)} %bitcast.10, ...), custom_call_target="tpu_custom_call" | custom-call | tf_op jit(solution)/shard_map/pallas_call | solution.py:775
  19.0 0.9 %shard_map.86 = (f32[256,128]{1,0:T(8,128)}, f32[256,128]{1,0:T(8,128)}, f32[1,3]{1,0:T(1,128)}) custom-call(f32[1,128]{1,0:T(1,128)S(1)} %get-tuple-element.10.all_totals, f32[256,128]{1,0:T(8,128)S(1)} %get-tuple-element.11.r0, f32[3,256,128]{2,1,0:T(8,128)S(1)} %get-tuple-element.12.fields, f32[3,256,128]{2,1,0:T(8,128)S(1)} %get-tuple-element.13.images), custom_call_target="tpu_custom_call" | custom-call | tf_op jit(solution)/shard_map/pallas_call | solution.py:840

commit v10 on v9

--- a/solution.py
+++ b/solution.py
@@ -332,10 +332,9 @@
         pl.semaphore_wait(barrier, n_all - 1)
 
         for_rows(lambda side: mini_copy(side).start())
-
+        for_rows(lambda side: row_copy(0, side).start())
         pl.when(gx == 0)(send_far_pack)
         for_sides(lambda side: col_copy(0, side).start())
-        for_rows(lambda side: row_copy(0, side).start())
         for_corners(lambda k: corner_copy(k).start(), True)
         for_sides(lambda side: edge_copy(side).start())
 

time: 20 us -> 20 us (level)
  no operation moved by 1% of the time
where the time goes in v10:
time: 20 us; the launch traced here: 19.9 us
  Pallas kernels  19.2 us (96%)
  between operations  0.64 us (3%)
    pallas_call x1, Pallas kernels, on_device(): pl.pallas_call(functools.partial(kernel, n_gx, n_gy, rows), out_shape=(ba...  18.4 us
    pallas_call x1, Pallas kernels, on_device(): pl.pallas_call(functools.partial(finish, total_cells), out_shape=(jax.Sha...  0.86 us

profile of v10, /device:TPU:0, one launch (start us, length us, event | category | flops | bytes accessed | tf_op | source)
XLA Modules:
  0.0 19.9 jit_solution(8581518411407729523)
XLA Ops:
  0.6 18.4 %shard_map.85 = (f32[3,256,128]{2,1,0:T(8,128)S(1)}, f32[3,256,128]{2,1,0:T(8,128)S(1)}, f32[1,128]{1,0:T(1,128)S(1)}, f32[256,128]{1,0:T(8,128)S(1)}) custom-call(s32[2,64]{1,0:T(2,128)} %edge_table.1, f32[256,128]{1,0:T(8,128)} %bitcast.7, f32[256,128]{1,0:T(8,128)} %bitcast.8, f32[256,128]{1,0:T(8,128)} %bitcast.9, f32[1,128]{1,0:T(1,128)} %bitcast.10, ...), custom_call_target="tpu_custom_call" | custom-call | tf_op jit(solution)/shard_map/pallas_call | solution.py:774
  19.0 0.9 %shard_map.86 = (f32[256,128]{1,0:T(8,128)}, f32[256,128]{1,0:T(8,128)}, f32[1,3]{1,0:T(1,128)}) custom-call(f32[1,128]{1,0:T(1,128)S(1)} %get-tuple-element.10.all_totals, f32[256,128]{1,0:T(8,128)S(1)} %get-tuple-element.11.r0, f32[3,256,128]{2,1,0:T(8,128)S(1)} %get-tuple-element.12.fields, f32[3,256,128]{2,1,0:T(8,128)S(1)} %get-tuple-element.13.images), custom_call_target="tpu_custom_call" | custom-call | tf_op jit(solution)/shard_map/pallas_call | solution.py:839

commit v11 on v10

--- a/solution.py
+++ b/solution.py
@@ -632,7 +632,6 @@
         if t == 0:
             prepare_weights(1)
             look_ahead()
-            pl.when(border & jnp.logical_not(last))(send_near)
         if t == 1:
             look_across()
         if t == 2:
@@ -651,7 +650,7 @@
         if t < ITERS - 1:
             send_rows(t + 1, jnp.concatenate([image[south_edge, :], image[north_edge, :]], 0))
         if t == 0:
-            pl.when(last)(send_near)
+            pl.when(border)(send_near)
         spaces.append(image)
     newest = len(spaces) - 1
     for i in range(len(spaces)):

time: 20 us -> 20 us (level)
  no operation moved by 1% of the time
where the time goes in v11:
time: 20 us; the launch traced here: 19.9 us
  Pallas kernels  19.2 us (96%)
  between operations  0.64 us (3%)
    pallas_call x1, Pallas kernels, on_device(): pl.pallas_call(functools.partial(kernel, n_gx, n_gy, rows), out_shape=(ba...  18.4 us
    pallas_call x1, Pallas kernels, on_device(): pl.pallas_call(functools.partial(finish, total_cells), out_shape=(jax.Sha...  0.86 us

profile of v11, /device:TPU:0, one launch (start us, length us, event | category | flops | bytes accessed | tf_op | source)
XLA Modules:
  0.0 19.9 jit_solution(8688358310989560418)
XLA Ops:
  0.6 18.4 %shard_map.85 = (f32[3,256,128]{2,1,0:T(8,128)S(1)}, f32[3,256,128]{2,1,0:T(8,128)S(1)}, f32[1,128]{1,0:T(1,128)S(1)}, f32[256,128]{1,0:T(8,128)S(1)}) custom-call(s32[2,64]{1,0:T(2,128)} %edge_table.1, f32[256,128]{1,0:T(8,128)} %bitcast.7, f32[256,128]{1,0:T(8,128)} %bitcast.8, f32[256,128]{1,0:T(8,128)} %bitcast.9, f32[1,128]{1,0:T(1,128)} %bitcast.10, ...), custom_call_target="tpu_custom_call" | custom-call | tf_op jit(solution)/shard_map/pallas_call | solution.py:773
  19.0 0.9 %shard_map.86 = (f32[256,128]{1,0:T(8,128)}, f32[256,128]{1,0:T(8,128)}, f32[1,3]{1,0:T(1,128)}) custom-call(f32[1,128]{1,0:T(1,128)S(1)} %get-tuple-element.10.all_totals, f32[256,128]{1,0:T(8,128)S(1)} %get-tuple-element.11.r0, f32[3,256,128]{2,1,0:T(8,128)S(1)} %get-tuple-element.12.fields, f32[3,256,128]{2,1,0:T(8,128)S(1)} %get-tuple-element.13.images), custom_call_target="tpu_custom_call" | custom-call | tf_op jit(solution)/shard_map/pallas_call | solution.py:838
